TPU v7x, 128 devices: a whole 4x4x4 slice. The times are simulated.
128 devices in a mesh: dp: 1, tp: 2 (over core), sp: 64 (over z, y, x).
Axes of the slice: x: 4, y: 4, z: 4, core: 2. Of those that a mesh axis runs over, the one named last changes fastest.
Arguments:
- hidden: bfloat16 [64, 8192], P('dp')
- lengths: int32 [64], P('dp')
- k_cache: bfloat16 [64, 1024, 8, 128], P('dp', 'sp', 'tp')
- v_cache: bfloat16 [64, 1024, 8, 128], P('dp', 'sp', 'tp')
- norm_gain: bfloat16 [8192], replicated
- w_query: bfloat16 [8192, 8192], P(None, 'tp')
- w_key: bfloat16 [8192, 1024], P(None, 'tp')
- w_value: bfloat16 [8192, 1024], P(None, 'tp')
- w_out: bfloat16 [8192, 8192], P('tp')
Outputs:
- output 1: bfloat16 [64, 8192], P('dp')
- output 2: bfloat16 [64, 1024, 8, 128], P('dp', 'sp', 'tp')
- output 3: bfloat16 [64, 1024, 8, 128], P('dp', 'sp', 'tp')
All inputs are finite; a program needn't handle non-finite values.
Results may differ from a plain program's by a relative error of at most 0.00421083.
Values sent between devices are 32-bit elements.
A program may use at most 1 GiB of HBM per device.

v0:
```python
import jax
import jax.numpy as jnp
from jax import lax
from jax.sharding import PartitionSpec as P

EPS = 1e-6
NEG_BIG = -1e30


def solution(mesh):
    cache_spec = P('dp', 'sp', 'tp', None)

    def local_step(hidden, lengths, k_cache, v_cache, norm_gain, w_query, w_key, w_value, w_out):
        batch, seq_block, kv_local, head_dim = k_cache.shape
        heads_local = w_query.shape[1] // head_dim
        group = heads_local // kv_local
        hid_f32 = hidden.astype(jnp.float32)
        inv_rms = lax.rsqrt(jnp.mean(hid_f32 * hid_f32, axis=-1, keepdims=True) + EPS)
        normed = (hid_f32 * inv_rms * norm_gain.astype(jnp.float32)).astype(jnp.bfloat16)
        query = jnp.dot(normed, w_query, preferred_element_type=jnp.float32).astype(jnp.bfloat16)
        query = query.reshape(batch, kv_local, group, head_dim)
        new_key = jnp.dot(normed, w_key, preferred_element_type=jnp.float32).astype(jnp.bfloat16)
        new_value = jnp.dot(normed, w_value, preferred_element_type=jnp.float32).astype(jnp.bfloat16)
        positions = lax.axis_index('sp') * seq_block + jnp.arange(seq_block)
        at_slot = (positions[None, :] == lengths[:, None])[:, :, None, None]
        k_new = jnp.where(at_slot, new_key.reshape(batch, 1, kv_local, head_dim), k_cache)
        v_new = jnp.where(at_slot, new_value.reshape(batch, 1, kv_local, head_dim), v_cache)
        scores = jnp.einsum('bkgd,btkd->bkgt', query, k_new, preferred_element_type=jnp.float32) * (head_dim ** -0.5)
        valid = (positions[None, :] <= lengths[:, None])[:, None, None, :]
        scores = jnp.where(valid, scores, NEG_BIG)
        local_peak = jnp.max(scores, axis=-1, keepdims=True)
        exp_vals = jnp.where(valid, jnp.exp(scores - local_peak), 0.0)
        local_denom = jnp.sum(exp_vals, axis=-1, keepdims=True)
        local_acc = jnp.einsum('bkgt,btkd->bkgd', exp_vals.astype(jnp.bfloat16), v_new, preferred_element_type=jnp.float32)
        global_peak = lax.pmax(local_peak, 'sp')
        rescale = jnp.exp(local_peak - global_peak)
        total_acc, total_denom = lax.psum((local_acc * rescale, local_denom * rescale), 'sp')
        attn_out = (total_acc / total_denom).astype(jnp.bfloat16).reshape(batch, heads_local * head_dim)
        part_out = jnp.dot(attn_out, w_out, preferred_element_type=jnp.float32)
        head_sum = lax.psum(part_out, 'tp')
        hidden_out = (hid_f32 + head_sum).astype(jnp.bfloat16)
        return hidden_out, k_new, v_new

    return jax.shard_map(
        local_step,
        mesh=mesh,
        in_specs=(P('dp', None), P('dp'), cache_spec, cache_spec, P(None), P(None, 'tp'), P(None, 'tp'), P(None, 'tp'), P('tp', None)),
        out_specs=(P('dp', None), cache_spec, cache_spec),
        check_vma=False,
    )
```

profile of v0, /device:TPU:1, one launch (start us, length us, event | category | flops | bytes accessed | tf_op | source)
XLA Modules:
  0.0 800.6 jit_solution(2771662199944600043)
XLA Ops:
  7.2 0.0 copy-start
  7.2 0.0 all-reduce.3.cloned.1.call-start
  7.2 1.6 fusion
  8.9 0.7 convert_element_type.28
  9.6 5.0 convolution_convert_fusion.2
  14.6 5.0 convolution_convert_fusion.1
  19.7 0.0 copy-start.3
  19.7 23.6 %fusion.5 = bf16[8,8,32,128]{3,1,2,0:T(8,128)(2,1)S(1)} fusion(bf16[8192,4096]{1,0:T(8,128)(2,1)} %param.14, bf16[64,8192]{1,0:T(8,128)(2,1)S(1)} %copy-done, f32[8192]{0:T(1024)S(1)} %convert_element_type.28, f32[64]{0:T(128)S(1)} %add_rsqrt_fusion), kind=kOutput, calls=%fused_computation.11 | convolution fusion | flops 4297326592 | bytes 68714752 | tf_op jit(solution)/shard_map/dot_general | solution.py:20
  43.3 0.1 copy.14
  43.4 0.1 broadcast_compare_fusion.1
  43.5 4.0 broadcast_select_fusion.1
  47.6 0.8 fusion.23
  48.4 296.4 %pmax.7 = f32[64,4,8,1]{2,1,0,3:T(4,128)S(1)} all-reduce(f32[64,4,8,1]{2,1,0,3:T(4,128)S(1)} %bitcast.27), channel_id=1, replica_groups=mesh['dp'=1,'tp'=2,'sp'=64] {'sp'}, use_global_device_ids=true, to_apply=%region_2.3 | all-reduce | flops 2048 | bytes 16384 | tf_op jit(solution)/shard_map/pmax | solution.py:35
  344.8 0.8 fusion.8
  345.5 0.1 fusion.17
  345.6 2.9 convolution_multiply_fusion
  348.5 0.0 all-reduce.3.cloned.1.call-update
  348.5 0.0 all-reduce.5.cloned.1.call-start
  348.6 286.3 %psum.22 = f32[64,4,8]{2,1,0:T(4,128)S(1)} all-reduce(f32[64,4,8]{2,1,0:T(4,128)S(1)} %get-tuple-element.3), channel_id=1, replica_groups=mesh['dp'=1,'tp'=2,'sp'=64] {'sp'}, use_global_device_ids=true, to_apply=%region_5.6 | all-reduce | flops 2048 | bytes 16384 | tf_op jit(solution)/shard_map/psum | solution.py:37
  634.9 1.6 divide_convert_fusion
  636.5 24.7 %fusion.11 = f32[64,8192]{1,0:T(8,128)} fusion(bf16[4096,8192]{1,0:T(8,128)(2,1)} %param.17, bf16[8,8,32,128]{3,2,1,0:T(8,128)(2,1)S(1)} %bitcast.25), kind=kOutput, calls=%fused_computation.22 | convolution fusion | flops 4294967296 | bytes 69730304 | tf_op jit(solution)/shard_map/dot_general | solution.py:39
  661.2 0.0 all-reduce.5.cloned.1.call-update
  661.2 129.8 %all-reduce.5.cloned.1.call-done = f32[64,8192]{1,0:T(8,128)} async-done(((f32[64,8192]{1,0:T(8,128)}), f32[64,8192]{1,0:T(8,128)}) %all-reduce.5.cloned.1.call-update) | async-done | bytes 2097168 | tf_op jit(solution)/shard_map/psum | solution.py:40
  791.0 2.7 fusion.3
  (11 shorter events, 0.1 us)
Async XLA Ops:
  7.2 2.4 copy-start
  7.2 627.7 %all-reduce.3.cloned.1.call-start = ((), (), s32[]{:S(2)}) async-start(), calls=%async_computation | async-start | bytes 2097152 | tf_op jit(solution)/shard_map/psum | solution.py:37
  19.7 23.8 %copy-start.3 = (s32[64]{0:T(128)S(1)}, s32[64]{0:T(128)}, u32[]{:S(2)}) copy-start(s32[64]{0:T(128)} %param.10) | copy-start | bytes 772
  19.7 23.8 %copy-start.2 = (bf16[64,16,4,128]{3,2,1,0:T(4,128)(2,1)S(1)}, bf16[64,16,4,128]{3,2,1,0:T(4,128)(2,1)}, u32[]{:S(2)}) copy-start(bf16[64,16,4,128]{3,2,1,0:T(4,128)(2,1)} %param.11) | copy-start | bytes 3145732
  47.6 298.0 %copy-start.1 = (bf16[64,16,4,128]{3,2,1,0:T(4,128)(2,1)}, bf16[64,16,4,128]{3,2,1,0:T(4,128)(2,1)S(1)}, u32[]{:S(2)}) copy-start(bf16[64,16,4,128]{3,2,1,0:T(4,128)(2,1)S(1)} %get-tuple-element.5) | copy-start | bytes 3145732
  348.5 442.5 %all-reduce.5.cloned.1.call-start = ((), (), s32[]{:S(2)}) async-start(), calls=%async_computation.1 | async-start | bytes 4194304 | tf_op jit(solution)/shard_map/psum | solution.py:40
Sparse Core Ops, SparseCore 0:
  348.7 177.4 all-reduce.2
  661.3 129.5 all-reduce.4
where the time goes:
time: 801 us
  blocking collectives  583 us (73%)
  waiting for transfers between devices  130 us (16%)
  matrix products  62.1 us (8%)
  between operations  14.2 us (2%)
  other arithmetic  11.6 us (1%)
    pmax x1, blocking collectives, local_step(): global_peak = lax.pmax(local_peak, 'sp')  296 us
    psum x1, blocking collectives, local_step(): lax.psum((local_acc * rescale, local_denom * rescale), 'sp')  286 us
    psum x1, waiting for transfers between devices, local_step(): head_sum = lax.psum(part_out, 'tp')  130 us
    dot_general x1, matrix products, local_step(): part_out = jnp.dot(attn_out, w_out, preferred_element_type=jnp.float32)  24.7 us
    dot_general x1, matrix products, local_step(): jnp.dot(normed, w_query, preferred_element_type=jnp.float32)  23.6 us
  transfers between devices with their start and end apart: 2, of which 1 were waited for; matrix products, arithmetic and copies ran while one was open for 0% of the time, Pallas kernels for 0%

commit v1 on v0

v1 whole, which is shorter than its diff:
```python
import functools

import jax
import jax.numpy as jnp
from jax import lax
from jax.experimental import pallas as pl
from jax.experimental.pallas import tpu as pltpu
from jax.sharding import PartitionSpec as P

EPS = 1e-6
NEG_BIG = -1e30
MESH = pl.DeviceIdType.MESH
F32, BF16 = jnp.float32, jnp.bfloat16

BATCH, D_MODEL, HEAD_DIM = 64, 8192, 128
KV, HEADS, GROUP = 4, 32, 8
SEQ = 16
STRIDE = (1, 4, 16)
TILES = (5, 5, 6)
OFFS = (0, 40, 80)
SLOTS, NCHUNK, CW = 11, 16, 512
GROUPS = ((24, 2, 2, 2), (0, 3, 2, 0), (12, 3, 2, 1), (2, 3, 1, 0), (14, 3, 1, 1), (32, 1, 1, 2), (36, 1, 1, 2))
AXES = (0, 1, 2)
LINE = (0, 1, 2, 3)
NEAR, FAR = (1, 3, 2), (2, 1, 3)


def kernel(lens, hid_h, gain_h, kc_h, vc_h, wq_h, wk_h, wv_h, wo_h,
           out_h, ko_h, vo_h,
           hid, gain, normed, kc, vc, qf, posm, acc, sfull,
           st_a, ra0, ra1, ra2, rst_a,
           b0_, b1_, b2_, st_b, rb0, rb1, rb2, rst_b,
           rc0, rc1, rc2, rst_c,
           attn, lhs, pout, pin, wbuf,
           in_sem, w_sem, out_sem, kv_sem,
           q_send, q_recv, a_send, a_recv, b_send, b_recv, c_send, c_recv,
           gb_send, gb_recv, ga_send, ga_recv, t_send, t_recv):
    sp = lax.axis_index("sp")
    tp = lax.axis_index("tp")
    coord = [sp % 4, (sp // 4) % 4, sp // 16]
    ra, redb, rb, rc = (ra0, ra1, ra2), (b0_, b1_, b2_), (rb0, rb1, rb2), (rc0, rc1, rc2)

    def peer(axis, r):
        c = coord[axis]
        t = (c + r) % 4
        return sp + (t - c) * STRIDE[axis], t

    c_hid = pltpu.make_async_copy(hid_h, hid, in_sem.at[0])
    c_gain = pltpu.make_async_copy(gain_h, gain, in_sem.at[1])
    c_hid.start()
    c_gain.start()
    x, y, z = coord

    def wcol(slot, half, hbm, col, width, at, sem):
        return pltpu.make_async_copy(
            hbm.at[pl.ds(half * 4096, 4096), pl.ds(pl.multiple_of(col, 128), width)],
            wbuf.at[slot, :, pl.ds(half * 256 + at, width)], sem)

    wq_copies = []
    chunks = (
        ((wq_h, (24 + 2 * z) * 128, 256, 0),),
        ((wq_h, (3 * x) * 128, 256, 0),),
        ((wq_h, (12 + 3 * y) * 128, 256, 0),),
        ((wq_h, (3 * x + 2) * 128, 128, 0), (wq_h, (12 + 3 * y + 2) * 128, 128, 128)),
        ((wk_h, z * 128, 128, 0), (wv_h, z * 128, 128, 128)),
    )
    nsem = 2
    for s, parts in enumerate(chunks):
        cs = []
        for half in range(2):
            for (hbm, col, width, at) in parts:
                cs.append(wcol(s, half, hbm, col, width, at, in_sem.at[nsem]))
                nsem += 1
        for c in cs:
            c.start()
        wq_copies.append(cs)
    c_k = pltpu.make_async_copy(kc_h, kc, kv_sem.at[0])
    c_v = pltpu.make_async_copy(vc_h, vc, kv_sem.at[1])
    c_k.start()
    c_v.start()

    barrier = pltpu.get_barrier_semaphore()
    for axis in AXES:
        for r in NEAR:
            pl.semaphore_signal(barrier, inc=1, device_id={"sp": peer(axis, r)[0]}, device_id_type=MESH)
    pl.semaphore_signal(barrier, inc=1, device_id={"tp": 1 - tp}, device_id_type=MESH)

    c_hid.wait()
    c_gain.wait()
    ss = jnp.zeros((BATCH, 128), F32)
    for c in range(0, D_MODEL, 512):
        h = hid[:, c:c + 512].astype(F32)
        h = h * h
        ss = ss + ((h[:, 0:128] + h[:, 128:256]) + (h[:, 256:384] + h[:, 384:512]))
    inv = lax.rsqrt(jnp.sum(ss, axis=1, keepdims=True) * (1.0 / D_MODEL) + EPS)
    for c in range(0, D_MODEL, 512):
        h = hid[:, c:c + 512].astype(F32)
        normed[:, c:c + 512] = (h * inv * gain[:, c:c + 512].astype(F32)).astype(BF16)

    def q_copy(g, r, own=True):
        base, mult, count, axis = GROUPS[g]
        c = coord[axis] if own else (coord[axis] + 4 - r) % 4
        rows = pl.ds(pl.multiple_of((base + mult * c) * BATCH, BATCH), count * BATCH)
        return pltpu.make_async_remote_copy(
            src_ref=qf.at[rows], dst_ref=qf.at[rows],
            send_sem=q_send.at[g, r - 1], recv_sem=q_recv.at[g, r - 1],
            device_id={"sp": peer(axis, r)[0]}, device_id_type=MESH)

    def wo_copy(j, slot):
        return pltpu.make_async_copy(
            wo_h.at[:, pl.ds(pl.multiple_of(j * CW, CW), CW)], wbuf.at[slot], w_sem.at[slot])

    def put(g, k, val):
        base, mult, count, axis = GROUPS[g]
        rows = pl.ds(pl.multiple_of((base + mult * coord[axis] + k) * BATCH, BATCH), BATCH)
        qf[rows, :] = val.astype(BF16).astype(F32)

    plan = (((0, 0), (0, 1)), ((1, 0), (1, 1)), ((2, 0), (2, 1)), ((3, 0), (4, 0)), ((5, 0), (6, 0)))
    for s in range(5):
        for c in wq_copies[s]:
            c.wait()
        if s == 4:
            for j in range(6):
                wo_copy(j, 5 + j).start()
        res = (jnp.dot(normed[:, 0:4096], wbuf[s, :, 0:256], preferred_element_type=F32)
               + jnp.dot(normed[:, 4096:8192], wbuf[s, :, 256:512], preferred_element_type=F32))
        (g0, k0), (g1, k1) = plan[s]
        put(g0, k0, res[:, 0:128])
        put(g1, k1, res[:, 128:256])
        if s == 0:
            pl.semaphore_wait(barrier, 10)
        for g in sorted({g0, g1}):
            for r in FAR:
                q_copy(g, r).start()
    for j in range(6, 11):
        wo_copy(j, j - 6).start()

    row = lax.broadcasted_iota(jnp.int32, (64, 128), 0)
    col = lax.broadcasted_iota(jnp.int32, (64, 128), 1)
    own = (row // 32 == col // 64) & ((row % 32) // GROUP == col % KV)
    posm[...] = jnp.where(own, sp * SEQ + (col % 64) // KV, 1 << 30)

    c_k.wait()
    c_v.wait()
    for g in range(7):
        for r in NEAR:
            q_copy(g, r, False).wait_recv()

    scale = HEAD_DIM ** -0.5
    rpos = sp * SEQ + lax.broadcasted_iota(jnp.int32, (64, 128), 0) // KV
    lane = lax.broadcasted_iota(jnp.int32, (8, 128), 1)
    UN = 4

    def attn_body(i, carry):
        lens_, qs, ks, vs = [], [], [], []
        for u in range(UN):
            b = (i * UN + u) * 2
            l0, l1 = lens[b], lens[b + 1]
            lens_.append((l0, l1))
            q = jnp.concatenate([qf[pl.ds(b, 32, stride=64), :], qf[pl.ds(b + 1, 32, stride=64), :]], axis=0)
            qs.append(q.astype(BF16))
            for ref, base, dst in ((kc, 32, ks), (vc, 36, vs)):
                both = []
                for e, ln in ((0, l0), (1, l1)):
                    new = qf[pl.ds(base * 64 + b + e, 4, stride=64), :]
                    new8 = jnp.concatenate([new, new], axis=0)
                    new64 = jnp.concatenate([new8] * 8, axis=0)
                    old = ref[pl.ds(pl.multiple_of((b + e) * 64, 64), 64), :]
                    both.append(jnp.where(rpos == ln, new64, old.astype(F32)).astype(BF16))
                val = jnp.concatenate(both, axis=0)
                ref[pl.ds(pl.multiple_of(b * 64, 128), 128), :] = val
                dst.append(val)
        ss_ = [lax.dot_general(qs[u], ks[u], (((1,), (1,)), ((), ())), preferred_element_type=F32) for u in range(UN)]
        ps, sts = [], []
        for u in range(UN):
            l0, l1 = lens_[u]
            pm = posm[...]
            valid = jnp.concatenate([pm[0:32] <= l0, pm[32:64] <= l1], axis=0)
            s = jnp.where(valid, ss_[u] * scale, NEG_BIG)
            m = jnp.max(s, axis=1, keepdims=True)
            e = jnp.where(valid, jnp.exp(s - m), 0.0)
            l = jnp.sum(e, axis=1, keepdims=True)
            ps.append(e.astype(BF16))
            col2 = lax.broadcasted_iota(jnp.int32, (64, 128), 1)
            sts.append(jnp.where(col2 < 64, m, l))
        for u in range(UN):
            b = (i * UN + u) * 2
            o = jnp.dot(ps[u], vs[u], preferred_element_type=F32)
            acc[pl.ds(b, 32, stride=64), :] = o[0:32]
            acc[pl.ds(b + 1, 32, stride=64), :] = o[32:64]
            sfull[pl.ds(b, 32, stride=64), :] = sts[u][0:32]
            sfull[pl.ds(b + 1, 32, stride=64), :] = sts[u][32:64]
        return carry

    lax.fori_loop(0, BATCH // 2 // UN, attn_body, 0)

    c_ko = pltpu.make_async_copy(kc, ko_h, kv_sem.at[0])
    c_vo = pltpu.make_async_copy(vc, vo_h, kv_sem.at[1])
    c_ko.start()
    c_vo.start()

    lane64 = lane % 64
    for c in AXES:
        n = TILES[c]
        for a in LINE:
            st = jnp.zeros((8, 128), F32)
            for p in LINE:
                for v in range(n):
                    r0 = (4 * a + p) * 128 + OFFS[c] + 8 * v
                    st = jnp.where(lane64 == p * n + v, sfull[r0:r0 + 8, :], st)
            st_a[c, a] = st

    def remote(src, dst, ss_sem, rs_sem, dev):
        return pltpu.make_async_remote_copy(
            src_ref=src, dst_ref=dst, send_sem=ss_sem, recv_sem=rs_sem,
            device_id={"sp": dev}, device_id_type=MESH)

    def copies_a(c, r):
        n = TILES[c]
        dev, t = peer(c, r)
        out = [remote(st_a.at[c, t], rst_a.at[c, r - 1], a_send.at[c, r - 1, 4], a_recv.at[c, r - 1, 4], dev)]
        for p in LINE:
            src = acc.at[pl.ds(pl.multiple_of(t * 512 + (p * 128 + OFFS[c]), 8), 8 * n)]
            out.append(remote(src, ra[c].at[r - 1, p], a_send.at[c, r - 1, p], a_recv.at[c, r - 1, p], dev))
        return out

    def copies_b(c, r):
        dev, t = peer((c + 1) % 3, r)
        return [remote(redb[c].at[t], rb[c].at[r - 1], b_send.at[c, r - 1, 0], b_recv.at[c, r - 1, 0], dev),
                remote(st_b.at[c, t], rst_b.at[c, r - 1], b_send.at[c, r - 1, 1], b_recv.at[c, r - 1, 1], dev)]

    def copies_c(c, r, own):
        axis = (c + 2) % 3
        dev, t = peer(axis, r)
        at = coord[axis] if own else (coord[axis] + 4 - r) % 4
        return [remote(rc[c].at[at], rc[c].at[at], c_send.at[c, r - 1, 0], c_recv.at[c, r - 1, 0], dev),
                remote(rst_c.at[c, at], rst_c.at[c, at], c_send.at[c, r - 1, 1], c_recv.at[c, r - 1, 1], dev)]

    def copy_gb(c, r, own):
        axis = (c + 1) % 3
        dev, t = peer(axis, r)
        at = coord[axis] if own else (coord[axis] + 4 - r) % 4
        rows = pl.ds(pl.multiple_of((4 * coord[c] + at) * 128 + OFFS[c], 8), 8 * TILES[c])
        return remote(attn.at[rows], attn.at[rows], gb_send.at[c, r - 1], gb_recv.at[c, r - 1], dev)

    def copies_ga(c, r, own):
        dev, t = peer(c, r)
        at = coord[c] if own else (coord[c] + 4 - r) % 4
        out = []
        for p in LINE:
            rows = pl.ds(pl.multiple_of((4 * at + p) * 128 + OFFS[c], 8), 8 * TILES[c])
            out.append(remote(attn.at[rows], attn.at[rows], ga_send.at[c, r - 1, p], ga_recv.at[c, r - 1, p], dev))
        return out

    for r in FAR:
        for c in AXES:
            for cp in copies_a(c, r):
                cp.start()

    def weights(stats):
        top = functools.reduce(jnp.maximum, stats)
        ws = [jnp.exp(s - top) for s in stats]
        l = sum(pltpu.roll(w, 64, 1) * s for w, s in zip(ws, stats))
        return top, ws, l

    def bc(w, j):
        return jnp.broadcast_to(w[:, j:j + 1], (8, 128))

    for c in AXES:
        n = TILES[c]
        for r in NEAR:
            for cp in copies_a(c, r):
                cp.wait_recv()
        a = coord[c]
        stats = [st_a[c, a]] + [rst_a[c, r] for r in AXES]
        top, ws, l = weights(stats)
        st = jnp.where(lane < 64, top, l)
        for p in LINE:
            for v in range(n):
                j = p * n + v
                o = bc(ws[0], j) * acc[pl.ds(pl.multiple_of(a * 512 + (p * 128 + OFFS[c] + 8 * v), 8), 8), :]
                for r in AXES:
                    o = o + bc(ws[r + 1], j) * ra[c][r, p, 8 * v:8 * v + 8, :]
                redb[c][p, 8 * v:8 * v + 8, :] = o
            st_b[c, p] = st if p == 0 else pltpu.roll(st, 128 - p * n, 1)
        for r in FAR:
            for cp in copies_b(c, r):
                cp.start()

    for c in AXES:
        n = TILES[c]
        for r in NEAR:
            for cp in copies_b(c, r):
                cp.wait_recv()
        b = coord[(c + 1) % 3]
        me = coord[(c + 2) % 3]
        stats = [st_b[c, b]] + [rst_b[c, r] for r in AXES]
        top, ws, l = weights(stats)
        for v in range(n):
            o = bc(ws[0], v) * redb[c][b, 8 * v:8 * v + 8, :]
            for r in AXES:
                o = o + bc(ws[r + 1], v) * rb[c][r, 8 * v:8 * v + 8, :]
            rc[c][me, 8 * v:8 * v + 8, :] = o
        rst_c[c, me] = jnp.where(lane < 64, top, l)
        for r in FAR:
            for cp in copies_c(c, r, True):
                cp.start()

    for c in AXES:
        n = TILES[c]
        for r in NEAR:
            for cp in copies_c(c, r, False):
                cp.wait_recv()
        stats = [rst_c[c, i] for i in LINE]
        top, ws, l = weights(stats)
        base = (4 * coord[c] + coord[(c + 1) % 3]) * 128 + OFFS[c]
        for v in range(n):
            o = bc(ws[0], v) * rc[c][0, 8 * v:8 * v + 8, :]
            for i in range(1, 4):
                o = o + bc(ws[i], v) * rc[c][i, 8 * v:8 * v + 8, :]
            o = o / bc(l, 64 + v)
            attn[pl.ds(pl.multiple_of(base + 8 * v, 8), 8), :] = o.astype(BF16).astype(F32)
        for r in FAR:
            copy_gb(c, r, True).start()

    for c in AXES:
        for r in NEAR:
            copy_gb(c, r, False).wait_recv()
        for r in FAR:
            for cp in copies_ga(c, r, True):
                cp.start()
    for c in AXES:
        for r in NEAR:
            for cp in copies_ga(c, r, False):
                cp.wait_recv()
    for h in range(HEADS):
        lhs[:, h * 128:(h + 1) * 128] = attn[h * 64:(h + 1) * 64, :].astype(BF16)

    def t_copy(j):
        return pltpu.make_async_remote_copy(
            src_ref=pout.at[j], dst_ref=pin.at[j], send_sem=t_send.at[j], recv_sem=t_recv.at[j],
            device_id={"tp": 1 - tp}, device_id_type=MESH)

    def out_copy(j):
        cols = pl.ds(pl.multiple_of(j * CW, CW), CW)
        return pltpu.make_async_copy(hid.at[:, cols], out_h.at[:, cols], out_sem.at[j])

    def finish(j):
        cols = pl.ds(pl.multiple_of(j * CW, CW), CW)
        t_copy(j).wait_recv()
        hid[:, cols] = (hid[:, cols].astype(F32) + (pout[j] + pin[j])).astype(BF16)
        out_copy(j).start()

    def fin(j, carry):
        slot = (j + 5) % SLOTS
        wo_copy(j, slot).wait()
        pout[j] = jnp.dot(lhs[...], wbuf[slot], preferred_element_type=F32)
        t_copy(j).start()

        @pl.when(j + SLOTS < NCHUNK)
        def _():
            wo_copy(j + SLOTS, slot).start()

        @pl.when(j > 0)
        def _():
            finish(j - 1)
        return carry

    lax.fori_loop(0, NCHUNK, fin, 0)
    finish(NCHUNK - 1)

    for g in range(7):
        for r in NEAR:
            q_copy(g, r).wait_send()
    for c in AXES:
        for r in NEAR:
            for cp in copies_a(c, r) + copies_b(c, r) + copies_c(c, r, True) + copies_ga(c, r, True):
                cp.wait_send()
            copy_gb(c, r, True).wait_send()
    c_ko.wait()
    c_vo.wait()

    def drain(j, carry):
        t_copy(j).wait_send()
        out_copy(j).wait()
        return carry
    lax.fori_loop(0, NCHUNK, drain, 0)


def solution(mesh):
    cache_spec = P('dp', 'sp', 'tp', None)

    def local_step(hidden, lengths, k_cache, v_cache, norm_gain, w_query, w_key, w_value, w_out):
        shape = k_cache.shape
        kc = k_cache.reshape(BATCH * SEQ * KV, HEAD_DIM)
        vc = v_cache.reshape(BATCH * SEQ * KV, HEAD_DIM)
        any_ = pl.BlockSpec(memory_space=pl.ANY)
        dma = pltpu.SemaphoreType.DMA
        V = pltpu.VMEM
        n8 = [8 * n for n in TILES]
        rows, half, wide = HEADS * BATCH, D_MODEL // 2, (BATCH, D_MODEL)
        stat = V((3, 4, 8, HEAD_DIM), F32)

        def vec(*lead):
            return [V((*lead, n, HEAD_DIM), F32) for n in n8]

        scratch = [
            V(wide, BF16), V((1, D_MODEL), BF16), V(wide, BF16), V(kc.shape, BF16), V(vc.shape, BF16),
            V((rows + 2 * KV * BATCH, HEAD_DIM), F32), V((BATCH, HEAD_DIM), jnp.int32),
            V((rows, HEAD_DIM), F32), V((rows, HEAD_DIM), F32),
            stat, *vec(3, 4), stat, *vec(4), stat, *vec(3), stat, *vec(4), stat,
            V((rows, HEAD_DIM), F32), V((BATCH, half), BF16),
            V((NCHUNK, BATCH, CW), F32), V((NCHUNK, BATCH, CW), F32), V((SLOTS, half, CW), BF16),
            dma((NCHUNK,)), dma((SLOTS,)), dma((NCHUNK,)), dma((2,)),
        ]
        for shape_ in ((7, 3), (3, 3, 5), (3, 3, 2), (3, 3, 2), (3, 3), (3, 3, 4), (NCHUNK,)):
            scratch += [dma(shape_), dma(shape_)]
        out, ko, vo = pl.pallas_call(
            kernel,
            out_shape=(jax.ShapeDtypeStruct((BATCH, D_MODEL), BF16),
                       jax.ShapeDtypeStruct(kc.shape, BF16), jax.ShapeDtypeStruct(vc.shape, BF16)),
            in_specs=[pl.BlockSpec(memory_space=pltpu.SMEM)] + [any_] * 8,
            out_specs=(any_, any_, any_),
            scratch_shapes=scratch,
            compiler_params=pltpu.CompilerParams(
                collective_id=0, has_side_effects=True, vmem_limit_bytes=67043328),
        )(lengths, hidden, norm_gain.reshape(1, D_MODEL), kc, vc, w_query, w_key, w_value, w_out)
        return out, ko.reshape(shape), vo.reshape(shape)

    return jax.shard_map(
        local_step,
        mesh=mesh,
        in_specs=(P('dp', None), P('dp'), cache_spec, cache_spec, P(None), P(None, 'tp'), P(None, 'tp'), P(None, 'tp'), P('tp', None)),
        out_specs=(P('dp', None), cache_spec, cache_spec),
        check_vma=False,
    )
```

time: 801 us -> 78.7 us (0.10)
  blocking collectives: 583 us -> 0 us
  waiting for transfers between devices: 130 us -> 0 us
  Pallas kernels: 0 us -> 68.8 us
  matrix products: 62.1 us -> 0 us
  between operations: 14.2 us -> 0.64 us
  other arithmetic: 11.6 us -> 0 us
  local copies, waits for them, and re-layouts: 0.15 us -> 8.94 us
    pmax x1 -> x0, blocking collectives: 296 us -> none  [local_step(): global_peak = lax.pmax(local_peak, 'sp')]
    psum x1 -> x0, blocking collectives: 286 us -> none  [local_step(): lax.psum((local_acc * rescale, local_denom * rescale), 'sp')]
    psum x2 -> x0, waiting for transfers between devices: 130 us -> none  [the longest x1 130 us: local_step(): head_sum = lax.psum(part_out, 'tp')]
    pallas_call x0 -> x1, Pallas kernels: none -> 68.8 us  [local_step(): pl.pallas_call(kernel, out_shape=(jax.ShapeDtypeStruct((BATCH, D_MODEL),...]
    dot_general x6 -> x0, matrix products: 62.1 us -> none  [the longest x1 24.7 us: local_step(): part_out = jnp.dot(attn_out, w_out, preferred_element_type=jnp.float32)]
  transfers between devices with their start and end apart: 2 -> 0, of which waited for: 1 -> 0; matrix products, arithmetic and copies ran while one was open for 0% -> 0% of each run, Pallas kernels for 0% -> 0%
where the time goes in v1:
time: 78.7 us; the launch traced here: 78.4 us
  Pallas kernels  68.8 us (87%)
  local copies, waits for them, and re-layouts  8.94 us (11%)
    pallas_call x1, Pallas kernels, local_step(): pl.pallas_call(kernel, out_shape=(jax.ShapeDtypeStruct((BATCH, D_MODEL),...  68.8 us
    unnamed x3, local copies, waits for them, and re-layouts  7.59 us

profile of v1, /device:TPU:1, one launch (start us, length us, event | category | flops | bytes accessed | tf_op | source)
XLA Modules:
  0.0 78.4 jit_solution(15877864348117497826)
XLA Ops:
  0.6 1.4 %reshape.21.gain_h = bf16[1,8192]{1,0:T(2,128)(2,1)} reshape(bf16[8192]{0:T(1024)(128)(2,1)} %param.13) | data formatting | bytes 32768 | tf_op jit(solution)/shard_map/reshape | solution.py:427
  2.0 68.8 %shard_map.112 = (bf16[64,8192]{1,0:T(8,128)(2,1)}, bf16[4096,128]{1,0:T(8,128)(2,1)}, bf16[4096,128]{1,0:T(8,128)(2,1)}) custom-call(s32[64]{0:T(128)} %lens.1, bf16[64,8192]{1,0:T(8,128)(2,1)} %hid_h.1, bf16[1,8192]{1,0:T(2,128)(2,1)} %reshape.21.gain_h, bf16[4096,128]{1,0:T(8,128)(2,1)} %bitcast.4, bf16[4096,128]{1,0:T(8,128)(2,1)} %bitcast.5, ...), custom_call_target="tpu_custom_call" | custom-call | tf_op jit(solution)/shard_map/pallas_call | solution.py:418
  70.8 2.3 %copy.15 = bf16[64,8192]{1,0:T(8,128)(2,1)} copy(bf16[64,8192]{1,0:T(8,128)(2,1)} %get-tuple-element.12) | data formatting | bytes 2097152
  73.1 2.7 %copy.16 = bf16[64,16,4,128]{3,2,1,0:T(4,128)(2,1)} copy(bf16[64,16,4,128]{3,2,1,0:T(4,128)(2,1)} %bitcast.7) | data formatting | bytes 2097152
  75.7 2.7 %copy.17 = bf16[64,16,4,128]{3,2,1,0:T(4,128)(2,1)} copy(bf16[64,16,4,128]{3,2,1,0:T(4,128)(2,1)} %bitcast.6) | data formatting | bytes 2097152

commit v2 on v1

--- a/solution.py
+++ b/solution.py
@@ -18,10 +18,11 @@
 STRIDE = (1, 4, 16)
 TILES = (5, 5, 6)
 OFFS = (0, 40, 80)
-SLOTS, NCHUNK, CW = 11, 16, 512
+SLOTS, NCHUNK, CW, LAG = 11, 16, 512, 3
 GROUPS = ((24, 2, 2, 2), (0, 3, 2, 0), (12, 3, 2, 1), (2, 3, 1, 0), (14, 3, 1, 1), (32, 1, 1, 2), (36, 1, 1, 2))
 AXES = (0, 1, 2)
 LINE = (0, 1, 2, 3)
+BLOCKS = 4
 NEAR, FAR = (1, 3, 2), (2, 1, 3)
 
 
@@ -92,10 +93,12 @@
         h = hid[:, c:c + 512].astype(F32)
         h = h * h
         ss = ss + ((h[:, 0:128] + h[:, 128:256]) + (h[:, 256:384] + h[:, 384:512]))
+    gf = gain[...].astype(F32)
     inv = lax.rsqrt(jnp.sum(ss, axis=1, keepdims=True) * (1.0 / D_MODEL) + EPS)
     for c in range(0, D_MODEL, 512):
         h = hid[:, c:c + 512].astype(F32)
-        normed[:, c:c + 512] = (h * inv * gain[:, c:c + 512].astype(F32)).astype(BF16)
+        g = jnp.concatenate([gf[k:k + 1] for k in range(c // HEAD_DIM, (c + 512) // HEAD_DIM)], axis=1)
+        normed[:, c:c + 512] = (h * inv * g).astype(BF16)
 
     def q_copy(g, r, own=True):
         base, mult, count, axis = GROUPS[g]
@@ -361,13 +364,14 @@
         def _():
             wo_copy(j + SLOTS, slot).start()
 
-        @pl.when(j > 0)
+        @pl.when(j >= LAG)
         def _():
-            finish(j - 1)
+            finish(j - LAG)
         return carry
 
     lax.fori_loop(0, NCHUNK, fin, 0)
-    finish(NCHUNK - 1)
+    for j in range(NCHUNK - LAG, NCHUNK):
+        finish(j)
 
     for g in range(7):
         for r in NEAR:
@@ -385,6 +389,25 @@
         out_copy(j).wait()
         return carry
     lax.fori_loop(0, NCHUNK, drain, 0)
+
+
+def copy_out(*refs):
+    n = (len(refs) - 2) // 3
+    ins, outs, bufs, i_sem, o_sem = refs[:n], refs[n:2 * n], refs[2 * n:3 * n], refs[-2], refs[-1]
+    moves = []
+    for k in range(n):
+        step = ins[k].shape[0] // BLOCKS
+        for j in range(BLOCKS):
+            rows = pl.ds(j * step, step)
+            moves.append((pltpu.make_async_copy(ins[k].at[rows], bufs[k].at[rows], i_sem.at[k, j]),
+                          pltpu.make_async_copy(bufs[k].at[rows], outs[k].at[rows], o_sem.at[k, j])))
+    for a, _ in moves:
+        a.start()
+    for a, b in moves:
+        a.wait()
+        b.start()
+    for _, b in moves:
+        b.wait()
 
 
 def solution(mesh):
@@ -405,7 +428,7 @@
             return [V((*lead, n, HEAD_DIM), F32) for n in n8]
 
         scratch = [
-            V(wide, BF16), V((1, D_MODEL), BF16), V(wide, BF16), V(kc.shape, BF16), V(vc.shape, BF16),
+            V(wide, BF16), V((D_MODEL // HEAD_DIM, HEAD_DIM), BF16), V(wide, BF16), V(kc.shape, BF16), V(vc.shape, BF16),
             V((rows + 2 * KV * BATCH, HEAD_DIM), F32), V((BATCH, HEAD_DIM), jnp.int32),
             V((rows, HEAD_DIM), F32), V((rows, HEAD_DIM), F32),
             stat, *vec(3, 4), stat, *vec(4), stat, *vec(3), stat, *vec(4), stat,
@@ -415,7 +438,7 @@
         ]
         for shape_ in ((7, 3), (3, 3, 5), (3, 3, 2), (3, 3, 2), (3, 3), (3, 3, 4), (NCHUNK,)):
             scratch += [dma(shape_), dma(shape_)]
-        out, ko, vo = pl.pallas_call(
+        res = pl.pallas_call(
             kernel,
             out_shape=(jax.ShapeDtypeStruct((BATCH, D_MODEL), BF16),
                        jax.ShapeDtypeStruct(kc.shape, BF16), jax.ShapeDtypeStruct(vc.shape, BF16)),
@@ -424,7 +447,14 @@
             scratch_shapes=scratch,
             compiler_params=pltpu.CompilerParams(
                 collective_id=0, has_side_effects=True, vmem_limit_bytes=67043328),
-        )(lengths, hidden, norm_gain.reshape(1, D_MODEL), kc, vc, w_query, w_key, w_value, w_out)
+        )(lengths, hidden, norm_gain.reshape(D_MODEL // HEAD_DIM, HEAD_DIM), kc, vc, w_query, w_key, w_value, w_out)
+        out, ko, vo = pl.pallas_call(
+            copy_out,
+            out_shape=tuple(jax.ShapeDtypeStruct(r.shape, r.dtype) for r in res),
+            in_specs=[any_] * len(res),
+            out_specs=(any_,) * len(res),
+            scratch_shapes=[V(r.shape, r.dtype) for r in res] + [dma((len(res), BLOCKS))] * 2,
+        )(*res)
         return out, ko.reshape(shape), vo.reshape(shape)
 
     return jax.shard_map(

time: 78.7 us -> 71.1 us (0.903)
  local copies, waits for them, and re-layouts: 8.94 us -> 0 us
  Pallas kernels: 68.8 us -> 70.3 us
    unnamed x3 -> x0, local copies, waits for them, and re-layouts: 7.59 us -> none
    pallas_call x0 -> x1, Pallas kernels: none -> 2.81 us  [local_step(): pl.pallas_call(copy_out, out_shape=tuple((jax.ShapeDtypeStruct(r.shape, r...]
    pallas_call x1, Pallas kernels: 68.8 us -> 67.5 us  [local_step(): pl.pallas_call(kernel, out_shape=(jax.ShapeDtypeStruct((BATCH, D_MODEL),...]
    reshape x1 -> x0, local copies, waits for them, and re-layouts: 1.35 us -> none  [local_step(): norm_gain.reshape(1, D_MODEL)]
where the time goes in v2:
time: 71.1 us; the launch traced here: 70.9 us
  Pallas kernels  70.3 us (99%)
    pallas_call x1, Pallas kernels, local_step(): pl.pallas_call(kernel, out_shape=(jax.ShapeDtypeStruct((BATCH, D_MODEL),...  67.5 us
    pallas_call x1, Pallas kernels, local_step(): pl.pallas_call(copy_out, out_shape=tuple((jax.ShapeDtypeStruct(r.shape, r...  2.81 us

profile of v2, /device:TPU:1, one launch (start us, length us, event | category | flops | bytes accessed | tf_op | source)
XLA Modules:
  0.0 70.9 jit_solution(2258882805215103661)
XLA Ops:
  0.6 67.5 %shard_map.112 = (bf16[64,8192]{1,0:T(8,128)(2,1)}, bf16[4096,128]{1,0:T(8,128)(2,1)}, bf16[4096,128]{1,0:T(8,128)(2,1)}) custom-call(s32[64]{0:T(128)} %lens.1, bf16[64,8192]{1,0:T(8,128)(2,1)} %hid_h.1, bf16[64,128]{1,0:T(8,128)(2,1)} %bitcast.7, bf16[4096,128]{1,0:T(8,128)(2,1)} %bitcast.5, bf16[4096,128]{1,0:T(8,128)(2,1)} %bitcast.6, ...), custom_call_target="tpu_custom_call" | custom-call | tf_op jit(solution)/shard_map/pallas_call | solution.py:441
  68.1 2.8 %shard_map.113 = (bf16[64,8192]{1,0:T(8,128)(2,1)}, bf16[4096,128]{1,0:T(8,128)(2,1)}, bf16[4096,128]{1,0:T(8,128)(2,1)}) custom-call(bf16[64,8192]{1,0:T(8,128)(2,1)} %get-tuple-element.9.refs_0_, bf16[4096,128]{1,0:T(8,128)(2,1)} %get-tuple-element.10.refs_1_, bf16[4096,128]{1,0:T(8,128)(2,1)} %get-tuple-element.11.refs_2_), custom_call_target="tpu_custom_call" | custom-call | tf_op jit(solution)/shard_map/pallas_call | solution.py:451

commit v3 on v2

--- a/solution.py
+++ b/solution.py
@@ -16,9 +16,13 @@
 KV, HEADS, GROUP = 4, 32, 8
 SEQ = 16
 STRIDE = (1, 4, 16)
-TILES = (5, 5, 6)
-OFFS = (0, 40, 80)
-SLOTS, NCHUNK, CW, LAG = 11, 16, 512, 3
+FIRST = (0, 12, 24)
+NH = (3, 3, 2)
+TILES = (6, 6, 4)
+SLOTS, CUTS, NCHUNK, CW = 11, 4, 16, 512
+WIDE = NCHUNK * CW // CUTS
+ORDER = (0, 1, 3, 2)
+BGROUP = 16
 GROUPS = ((24, 2, 2, 2), (0, 3, 2, 0), (12, 3, 2, 1), (2, 3, 1, 0), (14, 3, 1, 1), (32, 1, 1, 2), (36, 1, 1, 2))
 AXES = (0, 1, 2)
 LINE = (0, 1, 2, 3)
@@ -52,33 +56,33 @@
     c_gain.start()
     x, y, z = coord
 
-    def wcol(slot, half, hbm, col, width, at, sem):
-        return pltpu.make_async_copy(
-            hbm.at[pl.ds(half * 4096, 4096), pl.ds(pl.multiple_of(col, 128), width)],
-            wbuf.at[slot, :, pl.ds(half * 256 + at, width)], sem)
+    KB = 1024
+
+    def wcols(slot, hbm, col, width, at, base):
+        return [pltpu.make_async_copy(
+            hbm.at[pl.ds(k * KB, KB), pl.ds(pl.multiple_of(col, HEAD_DIM), width)],
+            wbuf.at[slot, :, pl.ds(k * 256 + at, width)], in_sem.at[base + k]) for k in range(D_MODEL // KB)]
 
     wq_copies = []
     chunks = (
-        ((wq_h, (24 + 2 * z) * 128, 256, 0),),
-        ((wq_h, (3 * x) * 128, 256, 0),),
-        ((wq_h, (12 + 3 * y) * 128, 256, 0),),
-        ((wq_h, (3 * x + 2) * 128, 128, 0), (wq_h, (12 + 3 * y + 2) * 128, 128, 128)),
-        ((wk_h, z * 128, 128, 0), (wv_h, z * 128, 128, 128)),
+        ((wq_h, 24 + 2 * z),),
+        ((wk_h, z), (wv_h, z)),
+        ((wq_h, 3 * x),),
+        ((wq_h, 12 + 3 * y),),
+        ((wq_h, 3 * x + 2), (wq_h, 12 + 3 * y + 2)),
     )
     nsem = 2
-    for s, parts in enumerate(chunks):
+    for i, parts in enumerate(chunks):
         cs = []
-        for half in range(2):
-            for (hbm, col, width, at) in parts:
-                cs.append(wcol(s, half, hbm, col, width, at, in_sem.at[nsem]))
-                nsem += 1
+        width = 256 // len(parts)
+        for k, (hbm, head) in enumerate(parts):
+            cs += wcols(i, hbm, head * HEAD_DIM, width, k * width, nsem)
+            nsem += D_MODEL // KB
         for c in cs:
             c.start()
         wq_copies.append(cs)
     c_k = pltpu.make_async_copy(kc_h, kc, kv_sem.at[0])
     c_v = pltpu.make_async_copy(vc_h, vc, kv_sem.at[1])
-    c_k.start()
-    c_v.start()
 
     barrier = pltpu.get_barrier_semaphore()
     for axis in AXES:
@@ -109,34 +113,48 @@
             send_sem=q_send.at[g, r - 1], recv_sem=q_recv.at[g, r - 1],
             device_id={"sp": peer(axis, r)[0]}, device_id_type=MESH)
 
-    def wo_copy(j, slot):
-        return pltpu.make_async_copy(
-            wo_h.at[:, pl.ds(pl.multiple_of(j * CW, CW), CW)], wbuf.at[slot], w_sem.at[slot])
+    def head0(c, r):
+        return FIRST[c] + NH[c] * ((coord[c] + 4 - r) % 4)
+
+    def wo_copies(i):
+        slot, r, at, out = (i + 5) % SLOTS, ORDER[i // CUTS], 0, []
+        for c in AXES:
+            n = NH[c] * HEAD_DIM
+            rows = pl.ds(pl.multiple_of(head0(c, r) * HEAD_DIM, HEAD_DIM), n)
+            out.append(pltpu.make_async_copy(
+                wo_h.at[rows, pl.ds((i % CUTS) * WIDE, WIDE)], wbuf.at[slot, pl.ds(at, n), :], w_sem.at[slot, c]))
+            at += n
+        return out
 
     def put(g, k, val):
         base, mult, count, axis = GROUPS[g]
         rows = pl.ds(pl.multiple_of((base + mult * coord[axis] + k) * BATCH, BATCH), BATCH)
         qf[rows, :] = val.astype(BF16).astype(F32)
 
-    plan = (((0, 0), (0, 1)), ((1, 0), (1, 1)), ((2, 0), (2, 1)), ((3, 0), (4, 0)), ((5, 0), (6, 0)))
-    for s in range(5):
-        for c in wq_copies[s]:
+    plan = (((0, 0), (0, 1)), ((5, 0), (6, 0)), ((1, 0), (1, 1)), ((2, 0), (2, 1)), ((3, 0), (4, 0)))
+    for i in range(5):
+        for c in wq_copies[i]:
             c.wait()
-        if s == 4:
+        if i == 2:
+            c_k.start()
+            c_v.start()
+        if i == 4:
             for j in range(6):
-                wo_copy(j, 5 + j).start()
-        res = (jnp.dot(normed[:, 0:4096], wbuf[s, :, 0:256], preferred_element_type=F32)
-               + jnp.dot(normed[:, 4096:8192], wbuf[s, :, 256:512], preferred_element_type=F32))
-        (g0, k0), (g1, k1) = plan[s]
-        put(g0, k0, res[:, 0:128])
-        put(g1, k1, res[:, 128:256])
-        if s == 0:
+                for c in wo_copies(j):
+                    c.start()
+        res = sum(jnp.dot(normed[:, k * KB:(k + 1) * KB], wbuf[i, :, k * 256:(k + 1) * 256], preferred_element_type=F32)
+                  for k in range(D_MODEL // KB))
+        (g0, k0), (g1, k1) = plan[i]
+        put(g0, k0, res[:, :HEAD_DIM])
+        put(g1, k1, res[:, HEAD_DIM:])
+        if i == 0:
             pl.semaphore_wait(barrier, 10)
         for g in sorted({g0, g1}):
             for r in FAR:
                 q_copy(g, r).start()
-    for j in range(6, 11):
-        wo_copy(j, j - 6).start()
+    for j in range(6, SLOTS):
+        for c in wo_copies(j):
+            c.start()
 
     row = lax.broadcasted_iota(jnp.int32, (64, 128), 0)
     col = lax.broadcasted_iota(jnp.int32, (64, 128), 1)
@@ -153,8 +171,24 @@
     rpos = sp * SEQ + lax.broadcasted_iota(jnp.int32, (64, 128), 0) // KV
     lane = lax.broadcasted_iota(jnp.int32, (8, 128), 1)
     UN = 4
-
-    def attn_body(i, carry):
+    acc3 = acc.reshape(HEADS, BATCH, HEAD_DIM)
+
+    def remote(src, dst, ss_sem, rs_sem, dev):
+        return pltpu.make_async_remote_copy(
+            src_ref=src, dst_ref=dst, send_sem=ss_sem, recv_sem=rs_sem,
+            device_id={"sp": dev}, device_id_type=MESH)
+
+    def copy_a(c, r, g):
+        dev, t = peer(c, r)
+        seqs = pl.ds(pl.multiple_of(g * BGROUP, BGROUP), BGROUP)
+        return remote(acc3.at[pl.ds(FIRST[c] + NH[c] * t, NH[c]), seqs], ra[c].at[r - 1, :, seqs],
+                      a_send.at[c, r - 1, g], a_recv.at[c, r - 1, g], dev)
+
+    def copy_sa(c, r):
+        dev, t = peer(c, r)
+        return remote(st_a.at[c, t], rst_a.at[c, r - 1], a_send.at[c, r - 1, 4], a_recv.at[c, r - 1, 4], dev)
+
+    def attn_part(i):
         lens_, qs, ks, vs = [], [], [], []
         for u in range(UN):
             b = (i * UN + u) * 2
@@ -193,9 +227,17 @@
             acc[pl.ds(b + 1, 32, stride=64), :] = o[32:64]
             sfull[pl.ds(b, 32, stride=64), :] = sts[u][0:32]
             sfull[pl.ds(b + 1, 32, stride=64), :] = sts[u][32:64]
+
+    def attn_body(g, carry):
+        per = BGROUP // 2 // UN
+        for k in range(per):
+            attn_part(g * per + k)
+        for r in FAR:
+            for c in AXES:
+                copy_a(c, r, g).start()
         return carry
 
-    lax.fori_loop(0, BATCH // 2 // UN, attn_body, 0)
+    lax.fori_loop(0, BATCH // BGROUP, attn_body, 0)
 
     c_ko = pltpu.make_async_copy(kc, ko_h, kv_sem.at[0])
     c_vo = pltpu.make_async_copy(vc, vo_h, kv_sem.at[1])
@@ -204,28 +246,12 @@
 
     lane64 = lane % 64
     for c in AXES:
-        n = TILES[c]
         for a in LINE:
             st = jnp.zeros((8, 128), F32)
-            for p in LINE:
-                for v in range(n):
-                    r0 = (4 * a + p) * 128 + OFFS[c] + 8 * v
-                    st = jnp.where(lane64 == p * n + v, sfull[r0:r0 + 8, :], st)
+            for j in range(8 * NH[c]):
+                r0 = (FIRST[c] + NH[c] * a) * BATCH + 8 * j
+                st = jnp.where(lane64 == j, sfull[r0:r0 + 8, :], st)
             st_a[c, a] = st
-
-    def remote(src, dst, ss_sem, rs_sem, dev):
-        return pltpu.make_async_remote_copy(
-            src_ref=src, dst_ref=dst, send_sem=ss_sem, recv_sem=rs_sem,
-            device_id={"sp": dev}, device_id_type=MESH)
-
-    def copies_a(c, r):
-        n = TILES[c]
-        dev, t = peer(c, r)
-        out = [remote(st_a.at[c, t], rst_a.at[c, r - 1], a_send.at[c, r - 1, 4], a_recv.at[c, r - 1, 4], dev)]
-        for p in LINE:
-            src = acc.at[pl.ds(pl.multiple_of(t * 512 + (p * 128 + OFFS[c]), 8), 8 * n)]
-            out.append(remote(src, ra[c].at[r - 1, p], a_send.at[c, r - 1, p], a_recv.at[c, r - 1, p], dev))
-        return out
 
     def copies_b(c, r):
         dev, t = peer((c + 1) % 3, r)
@@ -239,26 +265,21 @@
         return [remote(rc[c].at[at], rc[c].at[at], c_send.at[c, r - 1, 0], c_recv.at[c, r - 1, 0], dev),
                 remote(rst_c.at[c, at], rst_c.at[c, at], c_send.at[c, r - 1, 1], c_recv.at[c, r - 1, 1], dev)]
 
+    def piece(c, ra_, rb_):
+        b = (coord[(c + 1) % 3] + 4 - rb_) % 4
+        return pl.ds(pl.multiple_of(head0(c, ra_) * BATCH + b * (8 * TILES[c]), 8), 8 * TILES[c])
+
     def copy_gb(c, r, own):
-        axis = (c + 1) % 3
-        dev, t = peer(axis, r)
-        at = coord[axis] if own else (coord[axis] + 4 - r) % 4
-        rows = pl.ds(pl.multiple_of((4 * coord[c] + at) * 128 + OFFS[c], 8), 8 * TILES[c])
-        return remote(attn.at[rows], attn.at[rows], gb_send.at[c, r - 1], gb_recv.at[c, r - 1], dev)
-
-    def copies_ga(c, r, own):
-        dev, t = peer(c, r)
-        at = coord[c] if own else (coord[c] + 4 - r) % 4
-        out = []
-        for p in LINE:
-            rows = pl.ds(pl.multiple_of((4 * at + p) * 128 + OFFS[c], 8), 8 * TILES[c])
-            out.append(remote(attn.at[rows], attn.at[rows], ga_send.at[c, r - 1, p], ga_recv.at[c, r - 1, p], dev))
-        return out
+        rows = piece(c, 0, 0 if own else r)
+        return remote(attn.at[rows], attn.at[rows], gb_send.at[c, r - 1], gb_recv.at[c, r - 1], peer((c + 1) % 3, r)[0])
+
+    def copy_ga(c, r, q, own):
+        rows = piece(c, 0 if own else r, q)
+        return remote(attn.at[rows], attn.at[rows], ga_send.at[c, r - 1, q], ga_recv.at[c, r - 1, q], peer(c, r)[0])
 
     for r in FAR:
         for c in AXES:
-            for cp in copies_a(c, r):
-                cp.start()
+            copy_sa(c, r).start()
 
     def weights(stats):
         top = functools.reduce(jnp.maximum, stats)
@@ -272,19 +293,20 @@
     for c in AXES:
         n = TILES[c]
         for r in NEAR:
-            for cp in copies_a(c, r):
-                cp.wait_recv()
+            for g in range(BATCH // BGROUP):
+                copy_a(c, r, g).wait_recv()
+            copy_sa(c, r).wait_recv()
         a = coord[c]
         stats = [st_a[c, a]] + [rst_a[c, r] for r in AXES]
         top, ws, l = weights(stats)
         st = jnp.where(lane < 64, top, l)
+        for j in range(8 * NH[c]):
+            p, v, h, k = j // n, j % n, j // 8, j % 8
+            o = bc(ws[0], j) * acc[pl.ds(pl.multiple_of(head0(c, 0) * BATCH + 8 * j, 8), 8), :]
+            for r in AXES:
+                o = o + bc(ws[r + 1], j) * ra[c][r, h, 8 * k:8 * k + 8, :]
+            redb[c][p, 8 * v:8 * v + 8, :] = o
         for p in LINE:
-            for v in range(n):
-                j = p * n + v
-                o = bc(ws[0], j) * acc[pl.ds(pl.multiple_of(a * 512 + (p * 128 + OFFS[c] + 8 * v), 8), 8), :]
-                for r in AXES:
-                    o = o + bc(ws[r + 1], j) * ra[c][r, p, 8 * v:8 * v + 8, :]
-                redb[c][p, 8 * v:8 * v + 8, :] = o
             st_b[c, p] = st if p == 0 else pltpu.roll(st, 128 - p * n, 1)
         for r in FAR:
             for cp in copies_b(c, r):
@@ -316,7 +338,7 @@
                 cp.wait_recv()
         stats = [rst_c[c, i] for i in LINE]
         top, ws, l = weights(stats)
-        base = (4 * coord[c] + coord[(c + 1) % 3]) * 128 + OFFS[c]
+        base = piece(c, 0, 0).start
         for v in range(n):
             o = bc(ws[0], v) * rc[c][0, 8 * v:8 * v + 8, :]
             for i in range(1, 4):
@@ -325,19 +347,14 @@
             attn[pl.ds(pl.multiple_of(base + 8 * v, 8), 8), :] = o.astype(BF16).astype(F32)
         for r in FAR:
             copy_gb(c, r, True).start()
-
-    for c in AXES:
-        for r in NEAR:
-            copy_gb(c, r, False).wait_recv()
         for r in FAR:
-            for cp in copies_ga(c, r, True):
-                cp.start()
-    for c in AXES:
-        for r in NEAR:
-            for cp in copies_ga(c, r, False):
-                cp.wait_recv()
-    for h in range(HEADS):
-        lhs[:, h * 128:(h + 1) * 128] = attn[h * 64:(h + 1) * 64, :].astype(BF16)
+            copy_ga(c, r, 0, True).start()
+
+    for q in NEAR:
+        for c in AXES:
+            copy_gb(c, q, False).wait_recv()
+            for r in FAR:
+                copy_ga(c, r, q, True).start()
 
     def t_copy(j):
         return pltpu.make_async_remote_copy(
@@ -345,32 +362,46 @@
             device_id={"tp": 1 - tp}, device_id_type=MESH)
 
     def out_copy(j):
-        cols = pl.ds(pl.multiple_of(j * CW, CW), CW)
+        cols = pl.ds(j * CW, CW)
         return pltpu.make_async_copy(hid.at[:, cols], out_h.at[:, cols], out_sem.at[j])
 
     def finish(j):
-        cols = pl.ds(pl.multiple_of(j * CW, CW), CW)
+        cols = pl.ds(j * CW, CW)
         t_copy(j).wait_recv()
         hid[:, cols] = (hid[:, cols].astype(F32) + (pout[j] + pin[j])).astype(BF16)
         out_copy(j).start()
 
-    def fin(j, carry):
-        slot = (j + 5) % SLOTS
-        wo_copy(j, slot).wait()
-        pout[j] = jnp.dot(lhs[...], wbuf[slot], preferred_element_type=F32)
-        t_copy(j).start()
-
-        @pl.when(j + SLOTS < NCHUNK)
-        def _():
-            wo_copy(j + SLOTS, slot).start()
-
-        @pl.when(j >= LAG)
-        def _():
-            finish(j - LAG)
-        return carry
-
-    lax.fori_loop(0, NCHUNK, fin, 0)
-    for j in range(NCHUNK - LAG, NCHUNK):
+    per = NCHUNK // CUTS
+    for i in range(len(ORDER) * CUTS):
+        k, cc, slot = i // CUTS, i % CUTS, (i + 5) % SLOTS
+        r = ORDER[k]
+        if cc == 0:
+            if r > 0:
+                for c in AXES:
+                    for q in (0,) + NEAR:
+                        copy_ga(c, r, q, False).wait_recv()
+            at = 0
+            for c in AXES:
+                for h in range(NH[c]):
+                    rows = pl.ds(pl.multiple_of((head0(c, r) + h) * BATCH, BATCH), BATCH)
+                    lhs[k, :, at:at + HEAD_DIM] = attn[rows, :].astype(BF16)
+                    at += HEAD_DIM
+        for c in wo_copies(i):
+            c.wait()
+        for j in range(per * cc, per * cc + per):
+            at = (j % per) * CW
+            p = jnp.dot(lhs[k], wbuf[slot, :, at:at + CW], preferred_element_type=F32)
+            pout[j] = p if k == 0 else pout[j] + p
+        if k == CUTS - 1:
+            for j in range(per * cc, per * cc + per):
+                t_copy(j).start()
+            if cc > 0:
+                for j in range(per * cc - per, per * cc):
+                    finish(j)
+        if i + SLOTS < len(ORDER) * CUTS:
+            for c in wo_copies(i + SLOTS):
+                c.start()
+    for j in range(NCHUNK - per, NCHUNK):
         finish(j)
 
     for g in range(7):
@@ -378,9 +409,14 @@
             q_copy(g, r).wait_send()
     for c in AXES:
         for r in NEAR:
-            for cp in copies_a(c, r) + copies_b(c, r) + copies_c(c, r, True) + copies_ga(c, r, True):
+            for g in range(BATCH // BGROUP):
+                copy_a(c, r, g).wait_send()
+            copy_sa(c, r).wait_send()
+            for cp in copies_b(c, r) + copies_c(c, r, True):
                 cp.wait_send()
             copy_gb(c, r, True).wait_send()
+            for q in LINE:
+                copy_ga(c, r, q, True).wait_send()
     c_ko.wait()
     c_vo.wait()
 
@@ -431,10 +467,10 @@
             V(wide, BF16), V((D_MODEL // HEAD_DIM, HEAD_DIM), BF16), V(wide, BF16), V(kc.shape, BF16), V(vc.shape, BF16),
             V((rows + 2 * KV * BATCH, HEAD_DIM), F32), V((BATCH, HEAD_DIM), jnp.int32),
             V((rows, HEAD_DIM), F32), V((rows, HEAD_DIM), F32),
-            stat, *vec(3, 4), stat, *vec(4), stat, *vec(3), stat, *vec(4), stat,
-            V((rows, HEAD_DIM), F32), V((BATCH, half), BF16),
-            V((NCHUNK, BATCH, CW), F32), V((NCHUNK, BATCH, CW), F32), V((SLOTS, half, CW), BF16),
-            dma((NCHUNK,)), dma((SLOTS,)), dma((NCHUNK,)), dma((2,)),
+            stat, *[V((3, n, BATCH, HEAD_DIM), F32) for n in NH], stat, *vec(4), stat, *vec(3), stat, *vec(4), stat,
+            V((rows, HEAD_DIM), F32), V((len(ORDER), BATCH, half // len(ORDER)), BF16),
+            V((NCHUNK, BATCH, CW), F32), V((NCHUNK, BATCH, CW), F32), V((SLOTS, half // len(ORDER), WIDE), BF16),
+            dma((64,)), dma((SLOTS, 3)), dma((NCHUNK,)), dma((2,)),
         ]
         for shape_ in ((7, 3), (3, 3, 5), (3, 3, 2), (3, 3, 2), (3, 3), (3, 3, 4), (NCHUNK,)):
             scratch += [dma(shape_), dma(shape_)]

time: 71.1 us -> 66.4 us (0.934)
  Pallas kernels: 70.3 us -> 65.4 us
    pallas_call x1, Pallas kernels: 67.5 us -> 62.6 us  [local_step(): pl.pallas_call(kernel, out_shape=(jax.ShapeDtypeStruct((BATCH, D_MODEL),...]
where the time goes in v3:
time: 66.4 us; the launch traced here: 66.2 us
  Pallas kernels  65.4 us (98%)
  between operations  0.8 us (1%)
    pallas_call x1, Pallas kernels, local_step(): pl.pallas_call(kernel, out_shape=(jax.ShapeDtypeStruct((BATCH, D_MODEL),...  62.6 us
    pallas_call x1, Pallas kernels, local_step(): pl.pallas_call(copy_out, out_shape=tuple((jax.ShapeDtypeStruct(r.shape, r...  2.81 us

profile of v3, /device:TPU:1, one launch (start us, length us, event | category | flops | bytes accessed | tf_op | source)
XLA Modules:
  0.0 66.2 jit_solution(7622332070145396095)
XLA Ops:
  0.6 62.6 %shard_map.112 = (bf16[64,8192]{1,0:T(8,128)(2,1)}, bf16[4096,128]{1,0:T(8,128)(2,1)}, bf16[4096,128]{1,0:T(8,128)(2,1)}) custom-call(s32[64]{0:T(128)} %lens.1, bf16[64,8192]{1,0:T(8,128)(2,1)} %hid_h.1, bf16[64,128]{1,0:T(8,128)(2,1)} %bitcast.7, bf16[4096,128]{1,0:T(8,128)(2,1)} %bitcast.5, bf16[4096,128]{1,0:T(8,128)(2,1)} %bitcast.6, ...), custom_call_target="tpu_custom_call" | custom-call | tf_op jit(solution)/shard_map/pallas_call | solution.py:477
  63.2 2.8 %shard_map.113 = (bf16[64,8192]{1,0:T(8,128)(2,1)}, bf16[4096,128]{1,0:T(8,128)(2,1)}, bf16[4096,128]{1,0:T(8,128)(2,1)}) custom-call(bf16[64,8192]{1,0:T(8,128)(2,1)} %get-tuple-element.9.refs_0_, bf16[4096,128]{1,0:T(8,128)(2,1)} %get-tuple-element.10.refs_1_, bf16[4096,128]{1,0:T(8,128)(2,1)} %get-tuple-element.11.refs_2_), custom_call_target="tpu_custom_call" | custom-call | tf_op jit(solution)/shard_map/pallas_call | solution.py:487

commit v4 on v3

--- a/solution.py
+++ b/solution.py
@@ -34,12 +34,10 @@
            out_h, ko_h, vo_h,
            hid, gain, normed, kc, vc, qf, posm, acc, sfull,
            st_a, ra0, ra1, ra2, rst_a,
-           b0_, b1_, b2_, st_b, rb0, rb1, rb2, rst_b,
-           rc0, rc1, rc2, rst_c,
+           b0_, b1_, b2_, rb0, rb1, rb2, rc0, rc1, rc2,
            attn, lhs, pout, pin, wbuf,
-           in_sem, w_sem, out_sem, kv_sem,
-           q_send, q_recv, a_send, a_recv, b_send, b_recv, c_send, c_recv,
-           gb_send, gb_recv, ga_send, ga_recv, t_send, t_recv):
+           in_sem, w_sem, out_sem, kv_sem, sends,
+           q_recv, a_recv, sa_recv, b_recv, c_recv, gb_recv, ga_recv, t_recv):
     sp = lax.axis_index("sp")
     tp = lax.axis_index("tp")
     coord = [sp % 4, (sp // 4) % 4, sp // 16]
@@ -49,6 +47,14 @@
         c = coord[axis]
         t = (c + r) % 4
         return sp + (t - c) * STRIDE[axis], t
+
+    def remote(src, dst, ss_sem, rs_sem, dev):
+        return pltpu.make_async_remote_copy(
+            src_ref=src, dst_ref=dst, send_sem=ss_sem, recv_sem=rs_sem,
+            device_id={"sp": dev}, device_id_type=MESH)
+
+    def arrived(ref, sem):
+        remote(ref, ref, sem, sem, peer(0, 1)[0]).wait_recv()
 
     c_hid = pltpu.make_async_copy(hid_h, hid, in_sem.at[0])
     c_gain = pltpu.make_async_copy(gain_h, gain, in_sem.at[1])
@@ -58,12 +64,11 @@
 
     KB = 1024
 
-    def wcols(slot, hbm, col, width, at, base):
+    def wcols(slot, hbm, col, width, at):
         return [pltpu.make_async_copy(
             hbm.at[pl.ds(k * KB, KB), pl.ds(pl.multiple_of(col, HEAD_DIM), width)],
-            wbuf.at[slot, :, pl.ds(k * 256 + at, width)], in_sem.at[base + k]) for k in range(D_MODEL // KB)]
-
-    wq_copies = []
+            wbuf.at[slot, :, pl.ds(k * 256 + at, width)], in_sem.at[2 + slot]) for k in range(D_MODEL // KB)]
+
     chunks = (
         ((wq_h, 24 + 2 * z),),
         ((wk_h, z), (wv_h, z)),
@@ -71,16 +76,15 @@
         ((wq_h, 12 + 3 * y),),
         ((wq_h, 3 * x + 2), (wq_h, 12 + 3 * y + 2)),
     )
-    nsem = 2
     for i, parts in enumerate(chunks):
-        cs = []
         width = 256 // len(parts)
         for k, (hbm, head) in enumerate(parts):
-            cs += wcols(i, hbm, head * HEAD_DIM, width, k * width, nsem)
-            nsem += D_MODEL // KB
-        for c in cs:
-            c.start()
-        wq_copies.append(cs)
+            for c in wcols(i, hbm, head * HEAD_DIM, width, k * width):
+                c.start()
+
+    def slot_full(slot, sem):
+        pltpu.make_async_copy(wo_h.at[pl.ds(0, KB), pl.ds(0, WIDE)], wbuf.at[slot], sem).wait()
+
     c_k = pltpu.make_async_copy(kc_h, kc, kv_sem.at[0])
     c_v = pltpu.make_async_copy(vc_h, vc, kv_sem.at[1])
 
@@ -104,14 +108,10 @@
         g = jnp.concatenate([gf[k:k + 1] for k in range(c // HEAD_DIM, (c + 512) // HEAD_DIM)], axis=1)
         normed[:, c:c + 512] = (h * inv * g).astype(BF16)
 
-    def q_copy(g, r, own=True):
+    def q_copy(g, r):
         base, mult, count, axis = GROUPS[g]
-        c = coord[axis] if own else (coord[axis] + 4 - r) % 4
-        rows = pl.ds(pl.multiple_of((base + mult * c) * BATCH, BATCH), count * BATCH)
-        return pltpu.make_async_remote_copy(
-            src_ref=qf.at[rows], dst_ref=qf.at[rows],
-            send_sem=q_send.at[g, r - 1], recv_sem=q_recv.at[g, r - 1],
-            device_id={"sp": peer(axis, r)[0]}, device_id_type=MESH)
+        rows = pl.ds(pl.multiple_of((base + mult * coord[axis]) * BATCH, BATCH), count * BATCH)
+        return remote(qf.at[rows], qf.at[rows], sends.at[0], q_recv, peer(axis, r)[0])
 
     def head0(c, r):
         return FIRST[c] + NH[c] * ((coord[c] + 4 - r) % 4)
@@ -122,7 +122,7 @@
             n = NH[c] * HEAD_DIM
             rows = pl.ds(pl.multiple_of(head0(c, r) * HEAD_DIM, HEAD_DIM), n)
             out.append(pltpu.make_async_copy(
-                wo_h.at[rows, pl.ds((i % CUTS) * WIDE, WIDE)], wbuf.at[slot, pl.ds(at, n), :], w_sem.at[slot, c]))
+                wo_h.at[rows, pl.ds((i % CUTS) * WIDE, WIDE)], wbuf.at[slot, pl.ds(at, n), :], w_sem.at[slot]))
             at += n
         return out
 
@@ -133,12 +133,10 @@
 
     plan = (((0, 0), (0, 1)), ((5, 0), (6, 0)), ((1, 0), (1, 1)), ((2, 0), (2, 1)), ((3, 0), (4, 0)))
     for i in range(5):
-        for c in wq_copies[i]:
-            c.wait()
-        if i == 2:
+        slot_full(i, in_sem.at[2 + i])
+        if i == 4:
             c_k.start()
             c_v.start()
-        if i == 4:
             for j in range(6):
                 for c in wo_copies(j):
                     c.start()
@@ -163,9 +161,8 @@
 
     c_k.wait()
     c_v.wait()
-    for g in range(7):
-        for r in NEAR:
-            q_copy(g, r, False).wait_recv()
+    gathered = 3 * (HEADS + 2 * KV) * BATCH // 4
+    arrived(qf.at[pl.ds(0, gathered)], q_recv)
 
     scale = HEAD_DIM ** -0.5
     rpos = sp * SEQ + lax.broadcasted_iota(jnp.int32, (64, 128), 0) // KV
@@ -173,20 +170,15 @@
     UN = 4
     acc3 = acc.reshape(HEADS, BATCH, HEAD_DIM)
 
-    def remote(src, dst, ss_sem, rs_sem, dev):
-        return pltpu.make_async_remote_copy(
-            src_ref=src, dst_ref=dst, send_sem=ss_sem, recv_sem=rs_sem,
-            device_id={"sp": dev}, device_id_type=MESH)
-
     def copy_a(c, r, g):
         dev, t = peer(c, r)
         seqs = pl.ds(pl.multiple_of(g * BGROUP, BGROUP), BGROUP)
         return remote(acc3.at[pl.ds(FIRST[c] + NH[c] * t, NH[c]), seqs], ra[c].at[r - 1, :, seqs],
-                      a_send.at[c, r - 1, g], a_recv.at[c, r - 1, g], dev)
+                      sends.at[1], a_recv.at[c], dev)
 
     def copy_sa(c, r):
         dev, t = peer(c, r)
-        return remote(st_a.at[c, t], rst_a.at[c, r - 1], a_send.at[c, r - 1, 4], a_recv.at[c, r - 1, 4], dev)
+        return remote(st_a.at[c, t], rst_a.at[c, r - 1], sends.at[2], sa_recv.at[c], dev)
 
     def attn_part(i):
         lens_, qs, ks, vs = [], [], [], []
@@ -253,29 +245,26 @@
                 st = jnp.where(lane64 == j, sfull[r0:r0 + 8, :], st)
             st_a[c, a] = st
 
-    def copies_b(c, r):
+    def copy_b(c, r):
         dev, t = peer((c + 1) % 3, r)
-        return [remote(redb[c].at[t], rb[c].at[r - 1], b_send.at[c, r - 1, 0], b_recv.at[c, r - 1, 0], dev),
-                remote(st_b.at[c, t], rst_b.at[c, r - 1], b_send.at[c, r - 1, 1], b_recv.at[c, r - 1, 1], dev)]
-
-    def copies_c(c, r, own):
+        return remote(redb[c].at[t], rb[c].at[r - 1], sends.at[3], b_recv.at[c], dev)
+
+    def copy_c(c, r):
         axis = (c + 2) % 3
-        dev, t = peer(axis, r)
-        at = coord[axis] if own else (coord[axis] + 4 - r) % 4
-        return [remote(rc[c].at[at], rc[c].at[at], c_send.at[c, r - 1, 0], c_recv.at[c, r - 1, 0], dev),
-                remote(rst_c.at[c, at], rst_c.at[c, at], c_send.at[c, r - 1, 1], c_recv.at[c, r - 1, 1], dev)]
+        at = coord[axis]
+        return remote(rc[c].at[at], rc[c].at[at], sends.at[4], c_recv.at[c], peer(axis, r)[0])
 
     def piece(c, ra_, rb_):
         b = (coord[(c + 1) % 3] + 4 - rb_) % 4
         return pl.ds(pl.multiple_of(head0(c, ra_) * BATCH + b * (8 * TILES[c]), 8), 8 * TILES[c])
 
-    def copy_gb(c, r, own):
-        rows = piece(c, 0, 0 if own else r)
-        return remote(attn.at[rows], attn.at[rows], gb_send.at[c, r - 1], gb_recv.at[c, r - 1], peer((c + 1) % 3, r)[0])
-
-    def copy_ga(c, r, q, own):
-        rows = piece(c, 0 if own else r, q)
-        return remote(attn.at[rows], attn.at[rows], ga_send.at[c, r - 1, q], ga_recv.at[c, r - 1, q], peer(c, r)[0])
+    def copy_gb(c, r):
+        rows = piece(c, 0, 0)
+        return remote(attn.at[rows], attn.at[rows], sends.at[5], gb_recv.at[r - 1], peer((c + 1) % 3, r)[0])
+
+    def copy_ga(c, r, q):
+        rows = piece(c, 0, q)
+        return remote(attn.at[rows], attn.at[rows], sends.at[6], ga_recv.at[r - 1], peer(c, r)[0])
 
     for r in FAR:
         for c in AXES:
@@ -292,10 +281,8 @@
 
     for c in AXES:
         n = TILES[c]
-        for r in NEAR:
-            for g in range(BATCH // BGROUP):
-                copy_a(c, r, g).wait_recv()
-            copy_sa(c, r).wait_recv()
+        arrived(ra[c], a_recv.at[c])
+        arrived(rst_a.at[c], sa_recv.at[c])
         a = coord[c]
         stats = [st_a[c, a]] + [rst_a[c, r] for r in AXES]
         top, ws, l = weights(stats)
@@ -307,36 +294,30 @@
                 o = o + bc(ws[r + 1], j) * ra[c][r, h, 8 * k:8 * k + 8, :]
             redb[c][p, 8 * v:8 * v + 8, :] = o
         for p in LINE:
-            st_b[c, p] = st if p == 0 else pltpu.roll(st, 128 - p * n, 1)
+            redb[c][p, 8 * n:, :] = st if p == 0 else pltpu.roll(st, 128 - p * n, 1)
         for r in FAR:
-            for cp in copies_b(c, r):
-                cp.start()
+            copy_b(c, r).start()
 
     for c in AXES:
         n = TILES[c]
-        for r in NEAR:
-            for cp in copies_b(c, r):
-                cp.wait_recv()
+        arrived(rb[c], b_recv.at[c])
         b = coord[(c + 1) % 3]
         me = coord[(c + 2) % 3]
-        stats = [st_b[c, b]] + [rst_b[c, r] for r in AXES]
+        stats = [redb[c][b, 8 * n:, :]] + [rb[c][r, 8 * n:, :] for r in AXES]
         top, ws, l = weights(stats)
         for v in range(n):
             o = bc(ws[0], v) * redb[c][b, 8 * v:8 * v + 8, :]
             for r in AXES:
                 o = o + bc(ws[r + 1], v) * rb[c][r, 8 * v:8 * v + 8, :]
             rc[c][me, 8 * v:8 * v + 8, :] = o
-        rst_c[c, me] = jnp.where(lane < 64, top, l)
+        rc[c][me, 8 * n:, :] = jnp.where(lane < 64, top, l)
         for r in FAR:
-            for cp in copies_c(c, r, True):
-                cp.start()
+            copy_c(c, r).start()
 
     for c in AXES:
         n = TILES[c]
-        for r in NEAR:
-            for cp in copies_c(c, r, False):
-                cp.wait_recv()
-        stats = [rst_c[c, i] for i in LINE]
+        arrived(rc[c].at[pl.ds(0, 3)], c_recv.at[c])
+        stats = [rc[c][i, 8 * n:, :] for i in LINE]
         top, ws, l = weights(stats)
         base = piece(c, 0, 0).start
         for v in range(n):
@@ -346,85 +327,66 @@
             o = o / bc(l, 64 + v)
             attn[pl.ds(pl.multiple_of(base + 8 * v, 8), 8), :] = o.astype(BF16).astype(F32)
         for r in FAR:
-            copy_gb(c, r, True).start()
+            copy_gb(c, r).start()
         for r in FAR:
-            copy_ga(c, r, 0, True).start()
-
+            copy_ga(c, r, 0).start()
+
+    share = HEADS * BATCH // 4
     for q in NEAR:
+        arrived(attn.at[pl.ds(0, share // 4)], gb_recv.at[q - 1])
         for c in AXES:
-            copy_gb(c, q, False).wait_recv()
             for r in FAR:
-                copy_ga(c, r, q, True).start()
-
-    def t_copy(j):
+                copy_ga(c, r, q).start()
+
+    per = NCHUNK // CUTS
+
+    def t_copy(cc):
+        part = pl.ds(per * cc, per)
         return pltpu.make_async_remote_copy(
-            src_ref=pout.at[j], dst_ref=pin.at[j], send_sem=t_send.at[j], recv_sem=t_recv.at[j],
+            src_ref=pout.at[part], dst_ref=pin.at[part], send_sem=sends.at[7], recv_sem=t_recv.at[cc],
             device_id={"tp": 1 - tp}, device_id_type=MESH)
 
-    def out_copy(j):
-        cols = pl.ds(j * CW, CW)
-        return pltpu.make_async_copy(hid.at[:, cols], out_h.at[:, cols], out_sem.at[j])
-
-    def finish(j):
-        cols = pl.ds(j * CW, CW)
-        t_copy(j).wait_recv()
-        hid[:, cols] = (hid[:, cols].astype(F32) + (pout[j] + pin[j])).astype(BF16)
-        out_copy(j).start()
-
-    per = NCHUNK // CUTS
+    def finish(cc):
+        t_copy(cc).wait_recv()
+        for j in range(per * cc, per * cc + per):
+            cols = pl.ds(j * CW, CW)
+            hid[:, cols] = (hid[:, cols].astype(F32) + (pout[j] + pin[j])).astype(BF16)
+        cols = pl.ds(cc * WIDE, WIDE)
+        pltpu.make_async_copy(hid.at[:, cols], out_h.at[:, cols], out_sem).start()
+
     for i in range(len(ORDER) * CUTS):
         k, cc, slot = i // CUTS, i % CUTS, (i + 5) % SLOTS
         r = ORDER[k]
         if cc == 0:
             if r > 0:
-                for c in AXES:
-                    for q in (0,) + NEAR:
-                        copy_ga(c, r, q, False).wait_recv()
+                arrived(attn.at[pl.ds(0, share)], ga_recv.at[r - 1])
             at = 0
             for c in AXES:
                 for h in range(NH[c]):
                     rows = pl.ds(pl.multiple_of((head0(c, r) + h) * BATCH, BATCH), BATCH)
                     lhs[k, :, at:at + HEAD_DIM] = attn[rows, :].astype(BF16)
                     at += HEAD_DIM
-        for c in wo_copies(i):
-            c.wait()
+        slot_full(slot, w_sem.at[slot])
         for j in range(per * cc, per * cc + per):
             at = (j % per) * CW
             p = jnp.dot(lhs[k], wbuf[slot, :, at:at + CW], preferred_element_type=F32)
             pout[j] = p if k == 0 else pout[j] + p
         if k == CUTS - 1:
-            for j in range(per * cc, per * cc + per):
-                t_copy(j).start()
+            t_copy(cc).start()
             if cc > 0:
-                for j in range(per * cc - per, per * cc):
-                    finish(j)
+                finish(cc - 1)
         if i + SLOTS < len(ORDER) * CUTS:
             for c in wo_copies(i + SLOTS):
                 c.start()
-    for j in range(NCHUNK - per, NCHUNK):
-        finish(j)
-
-    for g in range(7):
-        for r in NEAR:
-            q_copy(g, r).wait_send()
-    for c in AXES:
-        for r in NEAR:
-            for g in range(BATCH // BGROUP):
-                copy_a(c, r, g).wait_send()
-            copy_sa(c, r).wait_send()
-            for cp in copies_b(c, r) + copies_c(c, r, True):
-                cp.wait_send()
-            copy_gb(c, r, True).wait_send()
-            for q in LINE:
-                copy_ga(c, r, q, True).wait_send()
+    finish(CUTS - 1)
+
+    strips = sum(TILES) * 8 + 3 * 8
+    for k, n in enumerate((gathered, 3 * share, 9 * 8, 3 * strips, 3 * strips, 3 * share // 4, 3 * share)):
+        remote(acc.at[pl.ds(0, n)], acc.at[pl.ds(0, n)], sends.at[k], sends.at[k], peer(0, 1)[0]).wait_send()
+    remote(pout, pin, sends.at[7], sends.at[7], peer(0, 1)[0]).wait_send()
     c_ko.wait()
     c_vo.wait()
-
-    def drain(j, carry):
-        t_copy(j).wait_send()
-        out_copy(j).wait()
-        return carry
-    lax.fori_loop(0, NCHUNK, drain, 0)
+    pltpu.make_async_copy(hid, out_h, out_sem).wait()
 
 
 def copy_out(*refs):
@@ -456,9 +418,8 @@
         any_ = pl.BlockSpec(memory_space=pl.ANY)
         dma = pltpu.SemaphoreType.DMA
         V = pltpu.VMEM
-        n8 = [8 * n for n in TILES]
+        n8 = [8 * n + 8 for n in TILES]
         rows, half, wide = HEADS * BATCH, D_MODEL // 2, (BATCH, D_MODEL)
-        stat = V((3, 4, 8, HEAD_DIM), F32)
 
         def vec(*lead):
             return [V((*lead, n, HEAD_DIM), F32) for n in n8]
@@ -467,13 +428,13 @@
             V(wide, BF16), V((D_MODEL // HEAD_DIM, HEAD_DIM), BF16), V(wide, BF16), V(kc.shape, BF16), V(vc.shape, BF16),
             V((rows + 2 * KV * BATCH, HEAD_DIM), F32), V((BATCH, HEAD_DIM), jnp.int32),
             V((rows, HEAD_DIM), F32), V((rows, HEAD_DIM), F32),
-            stat, *[V((3, n, BATCH, HEAD_DIM), F32) for n in NH], stat, *vec(4), stat, *vec(3), stat, *vec(4), stat,
+            V((3, 4, 8, HEAD_DIM), F32), *[V((3, n, BATCH, HEAD_DIM), F32) for n in NH], V((3, 3, 8, HEAD_DIM), F32),
+            *vec(4), *vec(3), *vec(4),
             V((rows, HEAD_DIM), F32), V((len(ORDER), BATCH, half // len(ORDER)), BF16),
             V((NCHUNK, BATCH, CW), F32), V((NCHUNK, BATCH, CW), F32), V((SLOTS, half // len(ORDER), WIDE), BF16),
-            dma((64,)), dma((SLOTS, 3)), dma((NCHUNK,)), dma((2,)),
+            dma((7,)), dma((SLOTS,)), dma, dma((2,)), dma((8,)),
+            dma, dma((3,)), dma((3,)), dma((3,)), dma((3,)), dma((3,)), dma((3,)), dma((CUTS,)),
         ]
-        for shape_ in ((7, 3), (3, 3, 5), (3, 3, 2), (3, 3, 2), (3, 3), (3, 3, 4), (NCHUNK,)):
-            scratch += [dma(shape_), dma(shape_)]
         res = pl.pallas_call(
             kernel,
             out_shape=(jax.ShapeDtypeStruct((BATCH, D_MODEL), BF16),

time: 66.4 us -> 65.3 us (0.983)
  Pallas kernels: 65.4 us -> 64.3 us
    pallas_call x1, Pallas kernels: 62.6 us -> 61.5 us  [local_step(): pl.pallas_call(kernel, out_shape=(jax.ShapeDtypeStruct((BATCH, D_MODEL),...]
where the time goes in v4:
time: 65.3 us; the launch traced here: 65.1 us
  Pallas kernels  64.3 us (98%)
  between operations  0.8 us (1%)
    pallas_call x1, Pallas kernels, local_step(): pl.pallas_call(kernel, out_shape=(jax.ShapeDtypeStruct((BATCH, D_MODEL),...  61.5 us
    pallas_call x1, Pallas kernels, local_step(): pl.pallas_call(copy_out, out_shape=tuple((jax.ShapeDtypeStruct(r.shape, r...  2.81 us

profile of v4, /device:TPU:1, one launch (start us, length us, event | category | flops | bytes accessed | tf_op | source)
XLA Modules:
  0.0 65.1 jit_solution(3284500130532610386)
XLA Ops:
  0.6 61.5 %shard_map.112 = (bf16[64,8192]{1,0:T(8,128)(2,1)}, bf16[4096,128]{1,0:T(8,128)(2,1)}, bf16[4096,128]{1,0:T(8,128)(2,1)}) custom-call(s32[64]{0:T(128)} %lens.1, bf16[64,8192]{1,0:T(8,128)(2,1)} %hid_h.1, bf16[64,128]{1,0:T(8,128)(2,1)} %bitcast.7, bf16[4096,128]{1,0:T(8,128)(2,1)} %bitcast.5, bf16[4096,128]{1,0:T(8,128)(2,1)} %bitcast.6, ...), custom_call_target="tpu_custom_call" | custom-call | tf_op jit(solution)/shard_map/pallas_call | solution.py:438
  62.2 2.8 %shard_map.113 = (bf16[64,8192]{1,0:T(8,128)(2,1)}, bf16[4096,128]{1,0:T(8,128)(2,1)}, bf16[4096,128]{1,0:T(8,128)(2,1)}) custom-call(bf16[64,8192]{1,0:T(8,128)(2,1)} %get-tuple-element.9.refs_0_, bf16[4096,128]{1,0:T(8,128)(2,1)} %get-tuple-element.10.refs_1_, bf16[4096,128]{1,0:T(8,128)(2,1)} %get-tuple-element.11.refs_2_), custom_call_target="tpu_custom_call" | custom-call | tf_op jit(solution)/shard_map/pallas_call | solution.py:448

commit v5 on v4

--- a/solution.py
+++ b/solution.py
@@ -22,6 +22,9 @@
 SLOTS, CUTS, NCHUNK, CW = 11, 4, 16, 512
 WIDE = NCHUNK * CW // CUTS
 ORDER = (0, 1, 3, 2)
+PIECES = ([(k, cc) for k in (0, 1) for cc in range(CUTS)]
+          + [(k, cc) for cc in range(CUTS) for k in (2, 3)])
+PAD = 128
 BGROUP = 16
 GROUPS = ((24, 2, 2, 2), (0, 3, 2, 0), (12, 3, 2, 1), (2, 3, 1, 0), (14, 3, 1, 1), (32, 1, 1, 2), (36, 1, 1, 2))
 AXES = (0, 1, 2)
@@ -83,7 +86,7 @@
                 c.start()
 
     def slot_full(slot, sem):
-        pltpu.make_async_copy(wo_h.at[pl.ds(0, KB), pl.ds(0, WIDE)], wbuf.at[slot], sem).wait()
+        pltpu.make_async_copy(wo_h.at[pl.ds(0, KB), pl.ds(0, WIDE)], wbuf.at[slot, :, pl.ds(0, WIDE)], sem).wait()
 
     c_k = pltpu.make_async_copy(kc_h, kc, kv_sem.at[0])
     c_v = pltpu.make_async_copy(vc_h, vc, kv_sem.at[1])
@@ -117,12 +120,12 @@
         return FIRST[c] + NH[c] * ((coord[c] + 4 - r) % 4)
 
     def wo_copies(i):
-        slot, r, at, out = (i + 5) % SLOTS, ORDER[i // CUTS], 0, []
+        slot, r, at, out = i % SLOTS, ORDER[PIECES[i][0]], 0, []
         for c in AXES:
             n = NH[c] * HEAD_DIM
             rows = pl.ds(pl.multiple_of(head0(c, r) * HEAD_DIM, HEAD_DIM), n)
             out.append(pltpu.make_async_copy(
-                wo_h.at[rows, pl.ds((i % CUTS) * WIDE, WIDE)], wbuf.at[slot, pl.ds(at, n), :], w_sem.at[slot]))
+                wo_h.at[rows, pl.ds(PIECES[i][1] * WIDE, WIDE)], wbuf.at[slot, pl.ds(at, n), pl.ds(0, WIDE)], w_sem.at[slot]))
             at += n
         return out
 
@@ -134,12 +137,9 @@
     plan = (((0, 0), (0, 1)), ((5, 0), (6, 0)), ((1, 0), (1, 1)), ((2, 0), (2, 1)), ((3, 0), (4, 0)))
     for i in range(5):
         slot_full(i, in_sem.at[2 + i])
-        if i == 4:
+        if i == 3:
             c_k.start()
             c_v.start()
-            for j in range(6):
-                for c in wo_copies(j):
-                    c.start()
         res = sum(jnp.dot(normed[:, k * KB:(k + 1) * KB], wbuf[i, :, k * 256:(k + 1) * 256], preferred_element_type=F32)
                   for k in range(D_MODEL // KB))
         (g0, k0), (g1, k1) = plan[i]
@@ -150,7 +150,9 @@
         for g in sorted({g0, g1}):
             for r in FAR:
                 q_copy(g, r).start()
-    for j in range(6, SLOTS):
+    c_k.wait()
+    c_v.wait()
+    for j in range(SLOTS):
         for c in wo_copies(j):
             c.start()
 
@@ -159,8 +161,6 @@
     own = (row // 32 == col // 64) & ((row % 32) // GROUP == col % KV)
     posm[...] = jnp.where(own, sp * SEQ + (col % 64) // KV, 1 << 30)
 
-    c_k.wait()
-    c_v.wait()
     gathered = 3 * (HEADS + 2 * KV) * BATCH // 4
     arrived(qf.at[pl.ds(0, gathered)], q_recv)
 
@@ -339,46 +339,69 @@
                 copy_ga(c, r, q).start()
 
     per = NCHUNK // CUTS
-
-    def t_copy(cc):
-        part = pl.ds(per * cc, per)
+    hp = per // 2
+
+    def t_copy(u):
+        part = pl.ds(hp * u, hp)
         return pltpu.make_async_remote_copy(
-            src_ref=pout.at[part], dst_ref=pin.at[part], send_sem=sends.at[7], recv_sem=t_recv.at[cc],
+            src_ref=pout.at[part], dst_ref=pin.at[part], send_sem=sends.at[7], recv_sem=t_recv.at[u],
             device_id={"tp": 1 - tp}, device_id_type=MESH)
 
-    def finish(cc):
-        t_copy(cc).wait_recv()
-        for j in range(per * cc, per * cc + per):
+    def finish(u):
+        t_copy(u).wait_recv()
+        for j in range(hp * u, hp * u + hp):
             cols = pl.ds(j * CW, CW)
             hid[:, cols] = (hid[:, cols].astype(F32) + (pout[j] + pin[j])).astype(BF16)
-        cols = pl.ds(cc * WIDE, WIDE)
+        cols = pl.ds(u * hp * CW, hp * CW)
         pltpu.make_async_copy(hid.at[:, cols], out_h.at[:, cols], out_sem).start()
 
-    for i in range(len(ORDER) * CUTS):
-        k, cc, slot = i // CUTS, i % CUTS, (i + 5) % SLOTS
-        r = ORDER[k]
-        if cc == 0:
-            if r > 0:
-                arrived(attn.at[pl.ds(0, share)], ga_recv.at[r - 1])
-            at = 0
-            for c in AXES:
-                for h in range(NH[c]):
-                    rows = pl.ds(pl.multiple_of((head0(c, r) + h) * BATCH, BATCH), BATCH)
-                    lhs[k, :, at:at + HEAD_DIM] = attn[rows, :].astype(BF16)
-                    at += HEAD_DIM
-        slot_full(slot, w_sem.at[slot])
-        for j in range(per * cc, per * cc + per):
-            at = (j % per) * CW
-            p = jnp.dot(lhs[k], wbuf[slot, :, at:at + CW], preferred_element_type=F32)
-            pout[j] = p if k == 0 else pout[j] + p
-        if k == CUTS - 1:
-            t_copy(cc).start()
-            if cc > 0:
-                finish(cc - 1)
-        if i + SLOTS < len(ORDER) * CUTS:
-            for c in wo_copies(i + SLOTS):
-                c.start()
-    finish(CUTS - 1)
+    def take(k):
+        r, at = ORDER[k], 0
+        if r > 0:
+            arrived(attn.at[pl.ds(0, share)], ga_recv.at[r - 1])
+        for c in AXES:
+            for h in range(NH[c]):
+                rows = pl.ds(pl.multiple_of((head0(c, r) + h) * BATCH, BATCH), BATCH)
+                lhs[k, :, at:at + HEAD_DIM] = attn[rows, :].astype(BF16)
+                at += HEAD_DIM
+
+    def part(i, j):
+        at = (j % per) * CW
+        return jnp.dot(lhs[PIECES[i][0]], wbuf[i % SLOTS, :, at:at + CW], preferred_element_type=F32)
+
+    for i in range(0, len(PIECES), 2):
+        pair = (i, i + 1)
+        if i in (0, CUTS):
+            take(i // CUTS)
+        if i == 2 * CUTS:
+            take(2)
+            take(3)
+        for e in pair:
+            slot_full(e % SLOTS, w_sem.at[e % SLOTS])
+        if i < 2 * CUTS:
+            for e in pair:
+                k, cc = PIECES[e]
+                for j in range(per * cc, per * cc + per):
+                    pout[j] = part(e, j) if k == 0 else pout[j] + part(e, j)
+        else:
+            cc = PIECES[i][1]
+            for u in (2 * cc, 2 * cc + 1):
+                for j in range(hp * u, hp * u + hp):
+                    pout[j] = pout[j] + (part(i, j) + part(i + 1, j))
+                if cc == CUTS - 1:
+                    t_copy(u).start()
+            if cc < CUTS - 1:
+                t_copy(2 * cc).start()
+                t_copy(2 * cc + 1).start()
+            if cc >= 2:
+                finish(2 * cc - 4)
+                finish(2 * cc - 3)
+        for e in pair:
+            if e + SLOTS < len(PIECES):
+                for c in wo_copies(e + SLOTS):
+                    c.start()
+    for u in range(2 * CUTS - 4, 2 * CUTS):
+        finish(u)
 
     strips = sum(TILES) * 8 + 3 * 8
     for k, n in enumerate((gathered, 3 * share, 9 * 8, 3 * strips, 3 * strips, 3 * share // 4, 3 * share)):
@@ -431,9 +454,9 @@
             V((3, 4, 8, HEAD_DIM), F32), *[V((3, n, BATCH, HEAD_DIM), F32) for n in NH], V((3, 3, 8, HEAD_DIM), F32),
             *vec(4), *vec(3), *vec(4),
             V((rows, HEAD_DIM), F32), V((len(ORDER), BATCH, half // len(ORDER)), BF16),
-            V((NCHUNK, BATCH, CW), F32), V((NCHUNK, BATCH, CW), F32), V((SLOTS, half // len(ORDER), WIDE), BF16),
+            V((NCHUNK, BATCH, CW), F32), V((NCHUNK, BATCH, CW), F32), V((SLOTS, half // len(ORDER), WIDE + PAD), BF16),
             dma((7,)), dma((SLOTS,)), dma, dma((2,)), dma((8,)),
-            dma, dma((3,)), dma((3,)), dma((3,)), dma((3,)), dma((3,)), dma((3,)), dma((CUTS,)),
+            dma, dma((3,)), dma((3,)), dma((3,)), dma((3,)), dma((3,)), dma((3,)), dma((2 * CUTS,)),
         ]
         res = pl.pallas_call(
             kernel,

time: 65.3 us -> 62.1 us (0.951)
  Pallas kernels: 64.3 us -> 61.1 us
    pallas_call x1, Pallas kernels: 61.5 us -> 58.3 us  [local_step(): pl.pallas_call(kernel, out_shape=(jax.ShapeDtypeStruct((BATCH, D_MODEL),...]
where the time goes in v5:
time: 62.1 us; the launch traced here: 61.9 us
  Pallas kernels  61.1 us (98%)
  between operations  0.8 us (1%)
    pallas_call x1, Pallas kernels, local_step(): pl.pallas_call(kernel, out_shape=(jax.ShapeDtypeStruct((BATCH, D_MODEL),...  58.3 us
    pallas_call x1, Pallas kernels, local_step(): pl.pallas_call(copy_out, out_shape=tuple((jax.ShapeDtypeStruct(r.shape, r...  2.81 us

profile of v5, /device:TPU:1, one launch (start us, length us, event | category | flops | bytes accessed | tf_op | source)
XLA Modules:
  0.0 61.9 jit_solution(15278328093250757582)
XLA Ops:
  0.6 58.3 %shard_map.112 = (bf16[64,8192]{1,0:T(8,128)(2,1)}, bf16[4096,128]{1,0:T(8,128)(2,1)}, bf16[4096,128]{1,0:T(8,128)(2,1)}) custom-call(s32[64]{0:T(128)} %lens.1, bf16[64,8192]{1,0:T(8,128)(2,1)} %hid_h.1, bf16[64,128]{1,0:T(8,128)(2,1)} %bitcast.7, bf16[4096,128]{1,0:T(8,128)(2,1)} %bitcast.5, bf16[4096,128]{1,0:T(8,128)(2,1)} %bitcast.6, ...), custom_call_target="tpu_custom_call" | custom-call | tf_op jit(solution)/shard_map/pallas_call | solution.py:461
  59.0 2.8 %shard_map.113 = (bf16[64,8192]{1,0:T(8,128)(2,1)}, bf16[4096,128]{1,0:T(8,128)(2,1)}, bf16[4096,128]{1,0:T(8,128)(2,1)}) custom-call(bf16[64,8192]{1,0:T(8,128)(2,1)} %get-tuple-element.9.refs_0_, bf16[4096,128]{1,0:T(8,128)(2,1)} %get-tuple-element.10.refs_1_, bf16[4096,128]{1,0:T(8,128)(2,1)} %get-tuple-element.11.refs_2_), custom_call_target="tpu_custom_call" | custom-call | tf_op jit(solution)/shard_map/pallas_call | solution.py:471

commit v6 on v5

--- a/solution.py
+++ b/solution.py
@@ -24,6 +24,7 @@
 ORDER = (0, 1, 3, 2)
 PIECES = ([(k, cc) for k in (0, 1) for cc in range(CUTS)]
           + [(k, cc) for cc in range(CUTS) for k in (2, 3)])
+PITCH = 72
 PAD = 128
 BGROUP = 16
 GROUPS = ((24, 2, 2, 2), (0, 3, 2, 0), (12, 3, 2, 1), (2, 3, 1, 0), (14, 3, 1, 1), (32, 1, 1, 2), (36, 1, 1, 2))
@@ -33,9 +34,9 @@
 NEAR, FAR = (1, 3, 2), (2, 1, 3)
 
 
-def kernel(lens, hid_h, gain_h, kc_h, vc_h, wq_h, wk_h, wv_h, wo_h,
+def kernel(lens_h, hid_h, gain_h, kc_h, vc_h, wq_h, wk_h, wv_h, wo_h,
            out_h, ko_h, vo_h,
-           hid, gain, normed, kc, vc, qf, posm, acc, sfull,
+           lens, hid, gain, normed, kc, vc, qf, posm, acc, sfull,
            st_a, ra0, ra1, ra2, rst_a,
            b0_, b1_, b2_, rb0, rb1, rb2, rc0, rc1, rc2,
            attn, lhs, pout, pin, wbuf,
@@ -61,6 +62,8 @@
 
     c_hid = pltpu.make_async_copy(hid_h, hid, in_sem.at[0])
     c_gain = pltpu.make_async_copy(gain_h, gain, in_sem.at[1])
+    c_len = pltpu.make_async_copy(lens_h, lens, kv_sem.at[2])
+    c_len.start()
     c_hid.start()
     c_gain.start()
     x, y, z = coord
@@ -111,10 +114,12 @@
         g = jnp.concatenate([gf[k:k + 1] for k in range(c // HEAD_DIM, (c + 512) // HEAD_DIM)], axis=1)
         normed[:, c:c + 512] = (h * inv * g).astype(BF16)
 
+    qf3 = qf.reshape(HEADS + 2 * KV, PITCH, HEAD_DIM)
+
     def q_copy(g, r):
         base, mult, count, axis = GROUPS[g]
-        rows = pl.ds(pl.multiple_of((base + mult * coord[axis]) * BATCH, BATCH), count * BATCH)
-        return remote(qf.at[rows], qf.at[rows], sends.at[0], q_recv, peer(axis, r)[0])
+        part = qf3.at[pl.ds(base + mult * coord[axis], count), pl.ds(0, BATCH)]
+        return remote(part, part, sends.at[0], q_recv.at[int(base >= HEADS)], peer(axis, r)[0])
 
     def head0(c, r):
         return FIRST[c] + NH[c] * ((coord[c] + 4 - r) % 4)
@@ -131,7 +136,7 @@
 
     def put(g, k, val):
         base, mult, count, axis = GROUPS[g]
-        rows = pl.ds(pl.multiple_of((base + mult * coord[axis] + k) * BATCH, BATCH), BATCH)
+        rows = pl.ds(pl.multiple_of((base + mult * coord[axis] + k) * PITCH, 8), BATCH)
         qf[rows, :] = val.astype(BF16).astype(F32)
 
     plan = (((0, 0), (0, 1)), ((5, 0), (6, 0)), ((1, 0), (1, 1)), ((2, 0), (2, 1)), ((3, 0), (4, 0)))
@@ -150,6 +155,7 @@
         for g in sorted({g0, g1}):
             for r in FAR:
                 q_copy(g, r).start()
+    c_len.wait()
     c_k.wait()
     c_v.wait()
     for j in range(SLOTS):
@@ -161,14 +167,31 @@
     own = (row // 32 == col // 64) & ((row % 32) // GROUP == col % KV)
     posm[...] = jnp.where(own, sp * SEQ + (col % 64) // KV, 1 << 30)
 
-    gathered = 3 * (HEADS + 2 * KV) * BATCH // 4
-    arrived(qf.at[pl.ds(0, gathered)], q_recv)
+    from_q, from_kv = 3 * HEADS * BATCH // 4, 6 * KV * BATCH // 4
+    arrived(qf.at[pl.ds(0, from_kv)], q_recv.at[1])
+    rpos = sp * SEQ + lax.broadcasted_iota(jnp.int32, (SEQ * KV, HEAD_DIM), 0) // KV
+
+    def place(i, carry):
+        for u in range(4):
+            b = i * 4 + u
+            hit = rpos == lens[b]
+            rows = pl.ds(pl.multiple_of(b * SEQ * KV, SEQ * KV), SEQ * KV)
+            for ref, base in ((kc, HEADS), (vc, HEADS + KV)):
+                new = qf[pl.ds(base * PITCH + b, KV, stride=PITCH), :]
+                ref[rows, :] = jnp.where(hit, jnp.concatenate([new] * SEQ, axis=0), ref[rows, :].astype(F32)).astype(BF16)
+        return carry
+
+    lax.fori_loop(0, BATCH // 4, place, 0)
+    c_ko = pltpu.make_async_copy(kc, ko_h, kv_sem.at[0])
+    c_vo = pltpu.make_async_copy(vc, vo_h, kv_sem.at[1])
+    c_ko.start()
+    c_vo.start()
+    arrived(qf.at[pl.ds(0, from_q)], q_recv.at[0])
 
     scale = HEAD_DIM ** -0.5
-    rpos = sp * SEQ + lax.broadcasted_iota(jnp.int32, (64, 128), 0) // KV
     lane = lax.broadcasted_iota(jnp.int32, (8, 128), 1)
     UN = 4
-    acc3 = acc.reshape(HEADS, BATCH, HEAD_DIM)
+    acc3 = acc.reshape(HEADS, PITCH, HEAD_DIM)
 
     def copy_a(c, r, g):
         dev, t = peer(c, r)
@@ -186,19 +209,11 @@
             b = (i * UN + u) * 2
             l0, l1 = lens[b], lens[b + 1]
             lens_.append((l0, l1))
-            q = jnp.concatenate([qf[pl.ds(b, 32, stride=64), :], qf[pl.ds(b + 1, 32, stride=64), :]], axis=0)
+            q = jnp.concatenate([qf[pl.ds(b, 32, stride=PITCH), :], qf[pl.ds(b + 1, 32, stride=PITCH), :]], axis=0)
             qs.append(q.astype(BF16))
-            for ref, base, dst in ((kc, 32, ks), (vc, 36, vs)):
-                both = []
-                for e, ln in ((0, l0), (1, l1)):
-                    new = qf[pl.ds(base * 64 + b + e, 4, stride=64), :]
-                    new8 = jnp.concatenate([new, new], axis=0)
-                    new64 = jnp.concatenate([new8] * 8, axis=0)
-                    old = ref[pl.ds(pl.multiple_of((b + e) * 64, 64), 64), :]
-                    both.append(jnp.where(rpos == ln, new64, old.astype(F32)).astype(BF16))
-                val = jnp.concatenate(both, axis=0)
-                ref[pl.ds(pl.multiple_of(b * 64, 128), 128), :] = val
-                dst.append(val)
+            rows = pl.ds(pl.multiple_of(b * SEQ * KV, 2 * SEQ * KV), 2 * SEQ * KV)
+            ks.append(kc[rows, :])
+            vs.append(vc[rows, :])
         ss_ = [lax.dot_general(qs[u], ks[u], (((1,), (1,)), ((), ())), preferred_element_type=F32) for u in range(UN)]
         ps, sts = [], []
         for u in range(UN):
@@ -215,10 +230,10 @@
         for u in range(UN):
             b = (i * UN + u) * 2
             o = jnp.dot(ps[u], vs[u], preferred_element_type=F32)
-            acc[pl.ds(b, 32, stride=64), :] = o[0:32]
-            acc[pl.ds(b + 1, 32, stride=64), :] = o[32:64]
-            sfull[pl.ds(b, 32, stride=64), :] = sts[u][0:32]
-            sfull[pl.ds(b + 1, 32, stride=64), :] = sts[u][32:64]
+            acc[pl.ds(b, 32, stride=PITCH), :] = o[0:32]
+            acc[pl.ds(b + 1, 32, stride=PITCH), :] = o[32:64]
+            sfull[pl.ds(b, 32, stride=PITCH), :] = sts[u][0:32]
+            sfull[pl.ds(b + 1, 32, stride=PITCH), :] = sts[u][32:64]
 
     def attn_body(g, carry):
         per = BGROUP // 2 // UN
@@ -231,17 +246,12 @@
 
     lax.fori_loop(0, BATCH // BGROUP, attn_body, 0)
 
-    c_ko = pltpu.make_async_copy(kc, ko_h, kv_sem.at[0])
-    c_vo = pltpu.make_async_copy(vc, vo_h, kv_sem.at[1])
-    c_ko.start()
-    c_vo.start()
-
     lane64 = lane % 64
     for c in AXES:
         for a in LINE:
             st = jnp.zeros((8, 128), F32)
             for j in range(8 * NH[c]):
-                r0 = (FIRST[c] + NH[c] * a) * BATCH + 8 * j
+                r0 = (FIRST[c] + NH[c] * a + j // 8) * PITCH + 8 * (j % 8)
                 st = jnp.where(lane64 == j, sfull[r0:r0 + 8, :], st)
             st_a[c, a] = st
 
@@ -289,7 +299,7 @@
         st = jnp.where(lane < 64, top, l)
         for j in range(8 * NH[c]):
             p, v, h, k = j // n, j % n, j // 8, j % 8
-            o = bc(ws[0], j) * acc[pl.ds(pl.multiple_of(head0(c, 0) * BATCH + 8 * j, 8), 8), :]
+            o = bc(ws[0], j) * acc[pl.ds(pl.multiple_of((head0(c, 0) + h) * PITCH + 8 * k, 8), 8), :]
             for r in AXES:
                 o = o + bc(ws[r + 1], j) * ra[c][r, h, 8 * k:8 * k + 8, :]
             redb[c][p, 8 * v:8 * v + 8, :] = o
@@ -404,7 +414,7 @@
         finish(u)
 
     strips = sum(TILES) * 8 + 3 * 8
-    for k, n in enumerate((gathered, 3 * share, 9 * 8, 3 * strips, 3 * strips, 3 * share // 4, 3 * share)):
+    for k, n in enumerate((from_q + from_kv, 3 * share, 9 * 8, 3 * strips, 3 * strips, 3 * share // 4, 3 * share)):
         remote(acc.at[pl.ds(0, n)], acc.at[pl.ds(0, n)], sends.at[k], sends.at[k], peer(0, 1)[0]).wait_send()
     remote(pout, pin, sends.at[7], sends.at[7], peer(0, 1)[0]).wait_send()
     c_ko.wait()
@@ -448,21 +458,21 @@
             return [V((*lead, n, HEAD_DIM), F32) for n in n8]
 
         scratch = [
-            V(wide, BF16), V((D_MODEL // HEAD_DIM, HEAD_DIM), BF16), V(wide, BF16), V(kc.shape, BF16), V(vc.shape, BF16),
-            V((rows + 2 * KV * BATCH, HEAD_DIM), F32), V((BATCH, HEAD_DIM), jnp.int32),
-            V((rows, HEAD_DIM), F32), V((rows, HEAD_DIM), F32),
+            pltpu.SMEM((BATCH,), jnp.int32), V(wide, BF16), V((D_MODEL // HEAD_DIM, HEAD_DIM), BF16), V(wide, BF16), V(kc.shape, BF16), V(vc.shape, BF16),
+            V(((HEADS + 2 * KV) * PITCH, HEAD_DIM), F32), V((BATCH, HEAD_DIM), jnp.int32),
+            V((HEADS * PITCH, HEAD_DIM), F32), V((HEADS * PITCH, HEAD_DIM), F32),
             V((3, 4, 8, HEAD_DIM), F32), *[V((3, n, BATCH, HEAD_DIM), F32) for n in NH], V((3, 3, 8, HEAD_DIM), F32),
             *vec(4), *vec(3), *vec(4),
             V((rows, HEAD_DIM), F32), V((len(ORDER), BATCH, half // len(ORDER)), BF16),
             V((NCHUNK, BATCH, CW), F32), V((NCHUNK, BATCH, CW), F32), V((SLOTS, half // len(ORDER), WIDE + PAD), BF16),
-            dma((7,)), dma((SLOTS,)), dma, dma((2,)), dma((8,)),
-            dma, dma((3,)), dma((3,)), dma((3,)), dma((3,)), dma((3,)), dma((3,)), dma((2 * CUTS,)),
+            dma((7,)), dma((SLOTS,)), dma, dma((3,)), dma((8,)),
+            dma((2,)), *[dma((3,))] * 6, dma((2 * CUTS,)),
         ]
         res = pl.pallas_call(
             kernel,
             out_shape=(jax.ShapeDtypeStruct((BATCH, D_MODEL), BF16),
                        jax.ShapeDtypeStruct(kc.shape, BF16), jax.ShapeDtypeStruct(vc.shape, BF16)),
-            in_specs=[pl.BlockSpec(memory_space=pltpu.SMEM)] + [any_] * 8,
+            in_specs=[any_] * 9,
             out_specs=(any_, any_, any_),
             scratch_shapes=scratch,
             compiler_params=pltpu.CompilerParams(

time: 62.1 us -> 60.2 us (0.969)
  Pallas kernels: 61.1 us -> 59.3 us
    pallas_call x1, Pallas kernels: 58.3 us -> 56.5 us  [local_step(): pl.pallas_call(kernel, out_shape=(jax.ShapeDtypeStruct((BATCH, D_MODEL),...]
where the time goes in v6:
time: 60.2 us; the launch traced here: 60.1 us
  Pallas kernels  59.3 us (99%)
  between operations  0.8 us (1%)
    pallas_call x1, Pallas kernels, local_step(): pl.pallas_call(kernel, out_shape=(jax.ShapeDtypeStruct((BATCH, D_MODEL),...  56.5 us
    pallas_call x1, Pallas kernels, local_step(): pl.pallas_call(copy_out, out_shape=tuple((jax.ShapeDtypeStruct(r.shape, r...  2.81 us

profile of v6, /device:TPU:1, one launch (start us, length us, event | category | flops | bytes accessed | tf_op | source)
XLA Modules:
  0.0 60.1 jit_solution(15738120831951947334)
XLA Ops:
  0.6 56.5 %shard_map.112 = (bf16[64,8192]{1,0:T(8,128)(2,1)}, bf16[4096,128]{1,0:T(8,128)(2,1)}, bf16[4096,128]{1,0:T(8,128)(2,1)}) custom-call(s32[64]{0:T(128)} %lens_h.1, bf16[64,8192]{1,0:T(8,128)(2,1)} %hid_h.1, bf16[64,128]{1,0:T(8,128)(2,1)} %bitcast.7, bf16[4096,128]{1,0:T(8,128)(2,1)} %bitcast.5, bf16[4096,128]{1,0:T(8,128)(2,1)} %bitcast.6, ...), custom_call_target="tpu_custom_call" | custom-call | tf_op jit(solution)/shard_map/pallas_call | solution.py:471
  57.1 2.8 %shard_map.113 = (bf16[64,8192]{1,0:T(8,128)(2,1)}, bf16[4096,128]{1,0:T(8,128)(2,1)}, bf16[4096,128]{1,0:T(8,128)(2,1)}) custom-call(bf16[64,8192]{1,0:T(8,128)(2,1)} %get-tuple-element.9.refs_0_, bf16[4096,128]{1,0:T(8,128)(2,1)} %get-tuple-element.10.refs_1_, bf16[4096,128]{1,0:T(8,128)(2,1)} %get-tuple-element.11.refs_2_), custom_call_target="tpu_custom_call" | custom-call | tf_op jit(solution)/shard_map/pallas_call | solution.py:481

commit v7 on v6

--- a/solution.py
+++ b/solution.py
@@ -338,14 +338,14 @@
             attn[pl.ds(pl.multiple_of(base + 8 * v, 8), 8), :] = o.astype(BF16).astype(F32)
         for r in FAR:
             copy_gb(c, r).start()
-        for r in FAR:
+        for r in NEAR:
             copy_ga(c, r, 0).start()
 
     share = HEADS * BATCH // 4
     for q in NEAR:
         arrived(attn.at[pl.ds(0, share // 4)], gb_recv.at[q - 1])
-        for c in AXES:
-            for r in FAR:
+        for r in NEAR:
+            for c in AXES:
                 copy_ga(c, r, q).start()
 
     per = NCHUNK // CUTS

time: 60.2 us -> 60.6 us (level)
  no operation moved by 1% of the time
where the time goes in v7:
time: 60.6 us; the launch traced here: 60.5 us
  Pallas kernels  59.7 us (99%)
  between operations  0.8 us (1%)
    pallas_call x1, Pallas kernels, local_step(): pl.pallas_call(kernel, out_shape=(jax.ShapeDtypeStruct((BATCH, D_MODEL),...  56.9 us
    pallas_call x1, Pallas kernels, local_step(): pl.pallas_call(copy_out, out_shape=tuple((jax.ShapeDtypeStruct(r.shape, r...  2.81 us

profile of v7, /device:TPU:1, one launch (start us, length us, event | category | flops | bytes accessed | tf_op | source)
XLA Modules:
  0.0 60.5 jit_solution(14213730899920736064)
XLA Ops:
  0.6 56.9 %shard_map.112 = (bf16[64,8192]{1,0:T(8,128)(2,1)}, bf16[4096,128]{1,0:T(8,128)(2,1)}, bf16[4096,128]{1,0:T(8,128)(2,1)}) custom-call(s32[64]{0:T(128)} %lens_h.1, bf16[64,8192]{1,0:T(8,128)(2,1)} %hid_h.1, bf16[64,128]{1,0:T(8,128)(2,1)} %bitcast.7, bf16[4096,128]{1,0:T(8,128)(2,1)} %bitcast.5, bf16[4096,128]{1,0:T(8,128)(2,1)} %bitcast.6, ...), custom_call_target="tpu_custom_call" | custom-call | tf_op jit(solution)/shard_map/pallas_call | solution.py:471
  57.5 2.8 %shard_map.113 = (bf16[64,8192]{1,0:T(8,128)(2,1)}, bf16[4096,128]{1,0:T(8,128)(2,1)}, bf16[4096,128]{1,0:T(8,128)(2,1)}) custom-call(bf16[64,8192]{1,0:T(8,128)(2,1)} %get-tuple-element.9.refs_0_, bf16[4096,128]{1,0:T(8,128)(2,1)} %get-tuple-element.10.refs_1_, bf16[4096,128]{1,0:T(8,128)(2,1)} %get-tuple-element.11.refs_2_), custom_call_target="tpu_custom_call" | custom-call | tf_op jit(solution)/shard_map/pallas_call | solution.py:481
